TPU v7x, 32 devices: a whole 2x2x4 slice. The times are simulated.
32 devices in a mesh: gx: 8 (over z, x), gy: 4 (over y, core).
Axes of the slice: x: 2, y: 2, z: 4, core: 2. Of those that a mesh axis runs over, the one named last changes fastest.
Arguments:
- displacement_old: float32 [3, 64, 64, 256], P(None, 'gx', 'gy'), may hold values from -6 to 6
- pressure_old: float32 [64, 64, 256], P('gx', 'gy'), may hold values from -6 to 6
- body_force: float32 [3, 64, 64, 256], P(None, 'gx', 'gy'), may hold values from -400 to 400
- fluid_source: float32 [64, 64, 256], P('gx', 'gy'), may hold values from -400 to 400
- material_ids: int32 [64, 64, 256], P('gx', 'gy'), may hold values from 0 to 7
- materials: float32 [5, 8], replicated, may hold values from 0.5 to 4
Outputs:
- displacement: float32 [3, 64, 64, 256], P(None, 'gx', 'gy')
- pressure: float32 [64, 64, 256], P('gx', 'gy')
All inputs are finite; a program needn't handle non-finite values.
Results may differ from a plain program's by a relative error of at most 0.00017.
Values sent between devices are 32-bit elements; how exact they have to be, the bound alone decides.
A program may use at most 64 MiB of HBM per device.

v0:
```python
import functools
import jax
import jax.numpy as jnp
from jax import lax
from jax.experimental import pallas as pl
from jax.experimental.pallas import tpu as pltpu
from jax.sharding import PartitionSpec as P

OUTER = 2
INNER = 3
step_time = 4.0
MESH = pl.DeviceIdType.MESH
F32 = jnp.float32


def kernel(dims, *refs):
    ngx, ngy, nx, ny, nz, nmat = dims
    (mat, d_hbm, p_hbm, bf_hbm, fs_hbm, ids_hbm, d_out, p_out,
     p_old, bforce, fsource, ids, lsem,
     XI, YIS, YIH, LAM, SHR, PRM, BIO, LAMY, SHRY, PRMY, BIOY, STO, STAB,
     SX, SY, SZ, SSUM, FX, FY, FZ, DIAG, PINV, HB, KF,
     PX, PYS, PYH, MX, MYS, MYH, MCS, MCH,
     WP, WM, AP, AD, DC, LY, LW, RB,
     isend, irecv, psend, precv, msend, mrecv, rsend, rrecv) = refs
    gx, gy = lax.axis_index("gx"), lax.axis_index("gy")
    has = {(-1, 0): gx > 0, (1, 0): gx < ngx - 1, (0, -1): gy > 0, (0, 1): gy < ngy - 1}
    has[(1, -1)] = jnp.logical_and(has[(1, 0)], has[(0, -1)])
    has[(-1, 1)] = jnp.logical_and(has[(-1, 0)], has[(0, 1)])

    rows = lax.broadcasted_iota(jnp.int32, (ny, nz), 0)
    lanes = lax.broadcasted_iota(jnp.int32, (ny, nz), 1)
    lanes8 = lax.broadcasted_iota(jnp.int32, (nx, nz), 1)
    rows8 = lax.broadcasted_iota(jnp.int32, (nx, nz), 0)
    lane1 = lax.broadcasted_iota(jnp.int32, (1, 128), 1)
    first_row, last_row = rows == 0, rows == ny - 1
    first_lane, last_lane = lanes == 0, lanes == nz - 1
    zero = jnp.zeros((ny, nz), F32)
    zero8 = jnp.zeros((nx, nz), F32)

    def upz(v):
        return pltpu.roll(v, nz - 1, 1)

    def dnz(v):
        return pltpu.roll(v, 1, 1)

    def upy(v, halo):
        return jnp.where(last_row, halo, pltpu.roll(v, ny - 1, 0))

    def dny(v, halo):
        return jnp.where(first_row, halo, pltpu.roll(v, 1, 0))

    def fold(v):
        out = None
        for i in range(0, ny, 8):
            for j in range(0, nz, 128):
                part = v[i:i + 8, j:j + 128]
                out = part if out is None else out + part
        return out

    def loop(body, init, low=0, high=nx, half=None):
        order = [low, high - 1] + list(range(low + 1, high - 1))
        for n, i in enumerate(order):
            init = body(i, init)
            if n == 1 and half is not None:
                half()
        return init

    def copies_of(pairs, send, recv):
        made = []
        for n, (src, dst, off) in enumerate(pairs):
            copy = pltpu.make_async_remote_copy(
                src_ref=src, dst_ref=dst, send_sem=send.at[n], recv_sem=recv.at[n],
                device_id=(gx + off[0], gy + off[1]), device_id_type=MESH)
            made.append((copy, off))
        return made

    def start(made, along=None):
        for copy, off in made:
            if along is not None and (off[0] != 0) != along:
                continue
            @pl.when(has[off])
            def _(copy=copy):
                copy.start()

    def wait_recv(made):
        for copy, off in made:
            @pl.when(has[(-off[0], -off[1])])
            def _(copy=copy):
                copy.wait_recv()

    def wait_send(made):
        for copy, off in made:
            @pl.when(has[off])
            def _(copy=copy):
                copy.wait_send()

    def scalar_field(f):
        return copies_of(
            [(PX.at[f, 1], PX.at[f, nx + 1], (-1, 0)), (PX.at[f, nx], PX.at[f, 0], (1, 0)),
             (PYS.at[f, 0], PYH.at[f, 1], (0, -1)), (PYS.at[f, 1], PYH.at[f, 0], (0, 1))],
            psend.at[f], precv.at[f])

    def vector_field(f):
        return copies_of(
            [(MX.at[f, :, 1], MX.at[f, :, nx + 1], (-1, 0)), (MX.at[f, :, nx], MX.at[f, :, 0], (1, 0)),
             (MYS.at[f, 0], MYH.at[f, 1], (0, -1)), (MYS.at[f, 1], MYH.at[f, 0], (0, 1)),
             (MCS.at[f, 0], MCH.at[f, 0], (1, -1)), (MCS.at[f, 1], MCH.at[f, 1], (-1, 1))],
            msend.at[f], mrecv.at[f])

    def put_scalar(f, i, v):
        PX[f, i + 1] = v
        PYS[f, 0, slice(i, i + 1), :] = v[0:1]
        PYS[f, 1, slice(i, i + 1), :] = v[ny - 1:ny]

    def put_vector(f, i, vs):
        for a in range(3):
            MX[f, a, i + 1] = vs[a]
            MYS[f, 0, a, slice(i, i + 1), :] = vs[a][0:1]
            MYS[f, 1, a, slice(i, i + 1), :] = vs[a][ny - 1:ny]

    def put_corners(f):
        MCS[f, 0] = MX[f, 1, nx, 0:1, :]
        MCS[f, 1] = MX[f, 0, 1, ny - 1:ny, :]

    local = [pltpu.make_async_copy(src, dst, lsem.at[n]) for n, (src, dst) in enumerate((
        (ids_hbm, ids), (p_hbm, PX.at[0, pl.ds(1, nx)]), (d_hbm, MX.at[0, :, pl.ds(1, nx)]),
        (p_hbm, p_old), (fs_hbm, fsource), (bf_hbm, bforce)))]
    for copy in local:
        copy.start()

    nf = 1 + OUTER * INNER
    XI[0] = jnp.zeros((ny, nz), jnp.int32)
    XI[nx + 1] = jnp.zeros((ny, nz), jnp.int32)
    for s in range(2):
        YIH[s] = jnp.zeros((nx, nz), jnp.int32)

    def clear(f, c):
        PX[f, 0] = zero
        PX[f, nx + 1] = zero
        for s in range(2):
            PYH[f, s] = zero8
            MCH[f, s] = jnp.zeros((1, nz), F32)
            for a in range(3):
                MX[f, a, s * (nx + 1)] = zero
                MYH[f, s, a] = zero8
        return c
    lax.fori_loop(0, nf, clear, 0)

    barrier = pltpu.get_barrier_semaphore()
    me, ndev = gx * ngy + gy, ngx * ngy

    def peer(d):
        t = lax.rem(me + d, ndev)
        return lax.div(t, ngy), lax.rem(t, ngy)
    for d in range(1, ndev):
        pl.semaphore_signal(barrier, inc=1, device_id=peer(d), device_id_type=MESH)

    def stage(i, c):
        code = ids[i] + 1
        XI[i + 1] = code
        YIS[0, slice(i, i + 1), :] = code[0:1]
        YIS[1, slice(i, i + 1), :] = code[ny - 1:ny]
        return c

    def stage_values(i, c):
        for side, y in ((0, 0), (1, ny - 1)):
            PYS[0, side, i:i + 1, :] = PX[0, i + 1, y:y + 1, :]
            for a in range(3):
                MYS[0, side, a, i:i + 1, :] = MX[0, a, i + 1, y:y + 1, :]
        return c
    local[0].wait()
    loop(stage, 0)
    local[1].wait()
    local[2].wait()
    loop(stage_values, 0)
    put_corners(0)
    pl.semaphore_wait(barrier, ndev - 1)

    codes_copy = copies_of(
        [(XI.at[1], XI.at[nx + 1], (-1, 0)), (XI.at[nx], XI.at[0], (1, 0)),
         (YIS.at[0], YIH.at[1], (0, -1)), (YIS.at[1], YIH.at[0], (0, 1))], isend, irecv)
    p_copy, d_copy = scalar_field(0), vector_field(0)
    start(codes_copy)
    start(p_copy)
    start(d_copy)

    def lookup(code, table_rows):
        out = [jnp.zeros(code.shape, F32) for _ in table_rows]
        for m in range(nmat):
            hit = code == m + 1
            out = [jnp.where(hit, mat[t, m], v) for t, v in zip(table_rows, out)]
        return out

    def look_plane(i, c):
        lam, shr, prm, sto, bio = lookup(XI[i + 1], (0, 1, 2, 3, 4))
        bio = 0.25 * bio
        LAM[i + 1] = lam
        SHR[i + 1] = shr
        PRM[i + 1] = prm
        BIO[i + 1] = bio
        STO[i] = sto
        STAB[i] = bio * bio / (lam + 2.0 / 3.0 * shr)
        return c
    loop(look_plane, 0)
    wait_recv(codes_copy)

    for j in (0, nx + 1):
        lam, shr, prm, bio = lookup(XI[j], (0, 1, 2, 4))
        LAM[j] = lam
        SHR[j] = shr
        PRM[j] = prm
        BIO[j] = 0.25 * bio
    for s in range(2):
        lam, shr, prm, bio = lookup(YIH[s], (0, 1, 2, 4))
        SHRY[s] = shr
        PRMY[s] = prm
        if s == 0:
            LAMY[...] = lam
            BIOY[...] = 0.25 * bio

    def harmonic(one, two):
        return (2.0 * step_time) * one * two / (one + two)

    def harmonic_plane(j, c):
        FX[j] = harmonic(PRM[j], PRM[j + 1])
        SX[j] = 0.5 * (SHR[j] + SHR[j + 1])
        return c
    loop(harmonic_plane, 0, 0, nx + 1)

    def coefs(i, c):
        shr, prm, lam = SHR[i + 1], PRM[i + 1], LAM[i + 1]
        row = slice(i, i + 1)
        fyu = harmonic(prm, upy(prm, PRMY[1, row, :]))
        fyd = harmonic(prm, dny(prm, PRMY[0, row, :]))
        fzu = jnp.where(last_lane, 0.0, harmonic(prm, upz(prm)))
        fzd = jnp.where(first_lane, 0.0, dnz(fzu))
        FY[1, i], FY[0, i], FZ[1, i], FZ[0, i] = fyu, fyd, fzu, fzd
        diag = STO[i] + STAB[i] + (FX[i] + FX[i + 1] + fyu + fyd + fzu + fzd)
        DIAG[i] = diag
        PINV[i] = 1.0 / diag
        half = 0.5 * shr
        syu = 0.5 * (shr + upy(shr, SHRY[1, row, :]))
        syd = 0.5 * (shr + dny(shr, SHRY[0, row, :]))
        szu = half + jnp.where(last_lane, 0.0, 0.5 * upz(shr))
        szd = half + jnp.where(first_lane, 0.0, 0.5 * dnz(shr))
        total = SX[i] + SX[i + 1] + syu + syd + szu + szd
        SY[1, i], SY[0, i] = syu, syd
        SZ[1, i] = jnp.where(last_lane, 0.0, szu)
        SZ[0, i] = jnp.where(first_lane, 0.0, szd)
        SSUM[i] = total
        h0 = 1.0 / (total + LAM[i])
        h1 = 1.0 / (total + dny(lam, LAMY[row, :]))
        h2 = 1.0 / (total + jnp.where(first_lane, 0.0, dnz(lam)))
        HB[0, i], HB[1, i], HB[2, i] = h0, h1, h2
        KF[i] = lam / (1.0 + lam * (h0 + h1 + h2))
        return c
    loop(coefs, 0)

    def apply_pressure(f, emit, init, half=None):
        def body(i, c):
            row = slice(i, i + 1)
            v = PX[f, i + 1]
            out = (DIAG[i] * v - FX[i + 1] * PX[f, i + 2] - FX[i] * PX[f, i]
                   - FY[1, i] * upy(v, PYH[f, 1, row, :]) - FY[0, i] * dny(v, PYH[f, 0, row, :])
                   - FZ[1, i] * upz(v) - FZ[0, i] * dnz(v))
            return emit(i, v, out, c)
        return loop(body, init, half=half)

    def apply_mech(f, emit, init, half=None):
        m = [MYH[f, 0, a] for a in range(3)]
        ahead = jnp.where(rows8 == nx - 1, MCH[f, 1], pltpu.roll(m[0], nx - 1, 0))
        z8 = jnp.where(lanes8 == nz - 1, 0.0, pltpu.roll(m[2], nz - 1, 1))
        LY[...] = LAMY[...] * (ahead - m[0] + MYS[f, 0, 1] - m[1] + z8 - m[2])
        m = [MX[f, a, 0] for a in range(3)]
        below_first = LAM[0] * (MX[f, 0, 1] - m[0] + upy(m[1], MCH[f, 0]) - m[1]
                          + jnp.where(last_lane, 0.0, upz(m[2])) - m[2])

        def weigh(i):
            w = [MX[f, a, i + 1] for a in range(3)]
            return LAM[i + 1] * (MX[f, 0, i + 2] - w[0] + upy(w[1], MYH[f, 1, 1, i:i + 1, :]) - w[1]
                                 + jnp.where(last_lane, 0.0, upz(w[2])) - w[2])

        def body(i, c):
            row = slice(i, i + 1)
            ws, outs, div = [], [], None
            for a in range(3):
                w, wx = MX[f, a, i + 1], MX[f, a, i + 2]
                wy, wz = upy(w, MYH[f, 1, a, row, :]), upz(w)
                out = (SSUM[i] * w - SX[i + 1] * wx - SX[i] * MX[f, a, i]
                       - SY[1, i] * wy - SY[0, i] * dny(w, MYH[f, 0, a, row, :])
                       - SZ[1, i] * wz - SZ[0, i] * dnz(w))
                part = (wx, wy, jnp.where(last_lane, 0.0, wz))[a] - w
                div = part if div is None else div + part
                ws.append(w)
                outs.append(out)
            weighted = LAM[i + 1] * div
            LW[i] = weighted
            before = below_first if i == 0 else weigh(i - 1) if i == nx - 1 else LW[i - 1]
            below = (before, dny(weighted, LY[row, :]), jnp.where(first_lane, 0.0, dnz(weighted)))
            outs = [outs[a] + (below[a] - weighted) for a in range(3)]
            return emit(i, ws, outs, c)
        return loop(body, init, half=half)

    def block_solve(i, r):
        scaled = [r[a] * HB[a, i] for a in range(3)]
        tail = KF[i] * (scaled[0] + scaled[1] + scaled[2])
        return [scaled[a] - HB[a, i] * tail for a in range(3)]

    def dot3(a, b):
        return fold(a[0] * b[0] + a[1] * b[1] + a[2] * b[2])

    summed = []

    def all_sum(q, sums):
        row = jnp.zeros((1, 128), F32)
        for k, s in enumerate(sums):
            row = jnp.where(lane1 == k, jnp.sum(s, keepdims=True), row)
        RB[q, me] = row
        made = []
        for d in sorted(range(1, ndev), key=lambda d: -min(d, ndev - d)):
            copy = pltpu.make_async_remote_copy(
                src_ref=RB.at[q, me], dst_ref=RB.at[q, me], send_sem=rsend.at[q, d],
                recv_sem=rrecv.at[q, d], device_id=peer(d), device_id_type=MESH)
            copy.start()
            made.append(copy)
        for copy in made:
            copy.wait_recv()
        summed.extend(made)
        parts = [RB[q, d] for d in range(ndev)]
        while len(parts) > 1:
            parts = [sum(parts[d + 1:d + 2], parts[d]) for d in range(0, len(parts), 2)]
        row = parts[0]
        return [row[:, k:k + 1] for k in range(len(sums))]

    def combine(t):
        n0, m0, m1, m2, m3, m4 = t
        n1 = m0 - n0
        n2 = m1 - n1
        l1, l2 = m1 / m0, m2 / m0
        d1 = m2 - l1 * m1
        e = m3 - l1 * m2
        l3 = jnp.where(d1 > 0, e / d1, 0.0)
        d2 = m4 - l2 * m2 - l3 * e
        y1 = n1 - l1 * n0
        y2 = n2 - l2 * n0 - l3 * y1
        c2 = jnp.where(d2 > 0, y2 / d2, 0.0)
        c1 = jnp.where(d1 > 0, y1 / d1, 0.0) - l3 * c2
        c0 = n0 / m0 - l1 * c1 - l2 * c2
        return c0, c1, c2

    zacc = jnp.zeros((8, 128), F32)
    wait_recv(p_copy)
    wait_send(p_copy)
    wait_send(codes_copy)

    def keep_ap(i, v, out, c):
        AP[i] = out
        return c
    apply_pressure(0, keep_ap, 0)

    def clear_change(i, c):
        DC[i] = zero
        return c
    loop(clear_change, 0)
    local[3].wait()
    local[4].wait()

    sent = []
    for outer in range(OUTER):
        base = 1 + INNER * outer

        def p_start(i, acc):
            if outer > 0:
                m_change(i, 0)
            rhs = (STO[i] * p_old[i] + step_time * fsource[i] - BIO[i + 1] * DC[i]
                   + STAB[i] * PX[0, i + 1])
            r = rhs - AP[i]
            u = r * PINV[i]
            put_scalar(base, i, u)
            return acc + fold(r * u)
        made = scalar_field(base)
        n0 = loop(p_start, zacc, half=functools.partial(start, made, True))
        start(made, False)
        sent.append(made)
        if outer > 0:
            loop(m_after, 0)
        if outer == 0:
            wait_recv(d_copy)
            wait_send(d_copy)

            def keep_ad(i, ws, outs, c):
                for a in range(3):
                    AD[a, i] = outs[a]
                return c
            apply_mech(0, keep_ad, 0)
            local[5].wait()
        sums = [n0]
        for k in range(INNER):
            sums = [jnp.sum(v, keepdims=True) for v in sums]
            wait_recv(made)

            def p_step(i, v, w, c):
                WP[k, i] = w
                even = c[0] + fold(v * w)
                if k == INNER - 1:
                    return (even,)
                u = w * PINV[i] - v
                put_scalar(base + k + 1, i, u)
                return even, c[1] + fold(u * w)
            half = None
            if k < INNER - 1:
                made = scalar_field(base + k + 1)
                half = functools.partial(start, made, True)
            sums += apply_pressure(base + k, p_step, (zacc,) * (1 if k == INNER - 1 else 2), half)
            if k < INNER - 1:
                start(made, False)
                sent.append(made)
        cs = combine(all_sum(2 * outer, sums))

        def p_update(j, c):
            v = PX[0, j]
            for k in range(INNER):
                v = v + cs[k] * PX[base + k, j]
            PX[0, j] = v
            return c
        loop(p_update, 0, 0, nx + 1)
        ph = PYH[0, 0]
        for k in range(INNER):
            ph = ph + cs[k] * PYH[base + k, 0]
        PYH[0, 0] = ph
        LY[...] = BIOY[...] * ph

        def m_start(i, acc):
            row = slice(i, i + 1)
            load = BIO[i + 1] * PX[0, i + 1]
            below = (BIO[i] * PX[0, i], dny(load, LY[row, :]), jnp.where(first_lane, 0.0, dnz(load)))
            r = [bforce[a, i] + (below[a] - load) - AD[a, i] for a in range(3)]
            u = block_solve(i, r)
            put_vector(base, i, u)
            return acc + dot3(r, u)
        made = vector_field(base)

        def send_planes(f, made):
            put_corners(f)
            start(made, True)
        n0 = loop(m_start, zacc, half=functools.partial(send_planes, base, made))
        start(made, False)
        sent.append(made)

        def p_after(i, c):
            if outer == OUTER - 1:
                p_out[i] = PX[0, i + 1]
            else:
                v = AP[i]
                for k in range(INNER):
                    v = v + cs[k] * WP[k, i]
                AP[i] = v
            return c
        loop(p_after, 0)
        sums = [n0]
        for k in range(INNER):
            sums = [jnp.sum(v, keepdims=True) for v in sums]
            wait_recv(made)

            def m_step(i, v, w, c):
                if outer < OUTER - 1:
                    for a in range(3):
                        WM[k, a, i] = w[a]
                even = c[0] + dot3(v, w)
                if k == INNER - 1:
                    return (even,)
                z = block_solve(i, w)
                u = [z[a] - v[a] for a in range(3)]
                put_vector(base + k + 1, i, u)
                return even, c[1] + dot3(u, w)
            half = None
            if k < INNER - 1:
                made = vector_field(base + k + 1)
                half = functools.partial(send_planes, base + k + 1, made)
            sums += apply_mech(base + k, m_step, (zacc,) * (1 if k == INNER - 1 else 2), half)
            if k < INNER - 1:
                start(made, False)
                sent.append(made)
        cs = combine(all_sum(2 * outer + 1, sums))

        def mixed(get, cs=cs, base=base):
            v = cs[0] * get(base)
            for k in range(1, INNER):
                v = v + cs[k] * get(base + k)
            return v

        def m_change(i, c):
            row = slice(i, i + 1)
            change = [mixed(lambda f, a=a: MX[f, a, i + 1]) for a in range(3)]
            cx = mixed(lambda f: MX[f, 0, i + 2])
            cy = upy(change[1], mixed(lambda f: MYH[f, 1, 1, row, :]))
            cz = jnp.where(last_lane, 0.0, upz(change[2]))
            DC[i] = DC[i] + (cx - change[0] + cy - change[1] + cz - change[2])
            return c

        def m_after(i, c, cs=cs, mixed=mixed, outer=outer):
            for a in range(3):
                before = MX[0, a, i + 1] if outer == 0 else d_out[a, i]
                d_out[a, i] = before + mixed(lambda f, a=a: MX[f, a, i + 1])
            if outer < OUTER - 1:
                for a in range(3):
                    v = AD[a, i]
                    for k in range(INNER):
                        v = v + cs[k] * WM[k, a, i]
                    AD[a, i] = v
            return c
        if outer == OUTER - 1:
            loop(m_after, 0)

    for made in sent:
        wait_send(made)
    for copy in summed:
        copy.wait_send()


def on_device(dims, d_old, p_old, bforce, fsource, ids, materials):
    ngx, ngy, nx, ny, nz, nmat = dims
    nf = 1 + OUTER * INNER
    nq = 2 * OUTER

    def vm(*shape, dtype=F32):
        return pltpu.VMEM(shape, dtype)
    plane, strip = (ny, nz), (nx, nz)
    cell = (nx, ny, nz)
    ext = (nx + 2, ny, nz)
    dma = pltpu.SemaphoreType.DMA
    scratch = [
        vm(*cell), vm(3, *cell), vm(*cell), vm(*cell, dtype=jnp.int32), dma((6,)),
        vm(*ext, dtype=jnp.int32), vm(2, *strip, dtype=jnp.int32), vm(2, *strip, dtype=jnp.int32),
        vm(*ext), vm(*ext), vm(*ext), vm(*ext), vm(*strip), vm(2, *strip), vm(2, *strip), vm(*strip),
        vm(*cell), vm(*cell),
        vm(nx + 1, *plane), vm(2, *cell), vm(2, *cell), vm(*cell),
        vm(nx + 1, *plane), vm(2, *cell), vm(2, *cell), vm(*cell), vm(*cell),
        vm(3, *cell), vm(*cell),
        vm(nf, *ext), vm(nf, 2, *strip), vm(nf, 2, *strip),
        vm(nf, 3, *ext), vm(nf, 2, 3, *strip), vm(nf, 2, 3, *strip), vm(nf, 2, 1, nz), vm(nf, 2, 1, nz),
        vm(INNER, *cell), vm(INNER, 3, *cell), vm(*cell), vm(3, *cell), vm(*cell),
        vm(*strip), vm(*cell), vm(nq, ngx * ngy, 1, 128),
        dma((4,)), dma((4,)), dma((nf, 4)), dma((nf, 4)), dma((nf, 6)), dma((nf, 6)),
        dma((nq, ngx * ngy)), dma((nq, ngx * ngy)),
    ]
    block = pl.BlockSpec(memory_space=pltpu.VMEM)
    return pl.pallas_call(
        functools.partial(kernel, dims),
        out_shape=(jax.ShapeDtypeStruct(d_old.shape, F32), jax.ShapeDtypeStruct(p_old.shape, F32)),
        in_specs=[pl.BlockSpec(memory_space=pltpu.SMEM)] + [pl.BlockSpec(memory_space=pl.ANY)] * 5,
        out_specs=(block, block),
        scratch_shapes=scratch,
        compiler_params=pltpu.CompilerParams(
            collective_id=0, has_side_effects=True, vmem_limit_bytes=63 * 1024 * 1024),
        name="poro",
    )(materials, d_old, p_old, bforce, fsource, ids)


def solution(mesh):
    ngx, ngy = mesh.shape["gx"], mesh.shape["gy"]

    def body(d_old, p_old, bforce, fsource, ids, materials):
        dims = (ngx, ngy, *p_old.shape, materials.shape[1])
        return on_device(dims, d_old, p_old, bforce, fsource, ids, materials)

    return jax.shard_map(
        body,
        mesh=mesh,
        in_specs=(P(None, "gx", "gy", None), P("gx", "gy", None), P(None, "gx", "gy", None),
                  P("gx", "gy", None), P("gx", "gy", None), P()),
        out_specs=(P(None, "gx", "gy", None), P("gx", "gy", None)),
        check_vma=False,
    )
```

profile of v0, /device:TPU:0, one launch (start us, length us, event | category | flops | bytes accessed | tf_op | source)
XLA Modules:
  0.0 85.8 jit_solution(4796176803451740282)
XLA Ops:
  0.6 82.7 %poro.1 = (f32[3,8,16,256]{3,2,1,0:T(8,128)}, f32[8,16,256]{2,1,0:T(8,128)}) custom-call(f32[5,8]{1,0:T(8,128)} %refs_0_.1, f32[3,8,16,256]{3,2,1,0:T(8,128)} %refs_1_.1, f32[8,16,256]{2,1,0:T(8,128)} %refs_2_.1, f32[3,8,16,256]{3,2,1,0:T(8,128)} %refs_3_.1, f32[8,16,256]{2,1,0:T(8,128)} %refs_4_.1, s32[8,16,256]{2,1,0:T(8,128)} %refs_5_.1), custom_call_target="tpu_custom_call" | custom-call | tf_op jit(solution)/shard_map/poro/pallas_call | solution.py:548
  83.3 0.0 copy-start
  83.3 1.8 %copy.10 = f32[3,8,16,256]{3,2,1,0:T(8,128)} copy(f32[3,8,16,256]{3,2,1,0:T(8,128)} %get-tuple-element.4) | data formatting | bytes 786432
  85.1 0.0 copy-done
  85.1 0.7 copy.11
Async XLA Ops:
  83.3 1.8 %copy-start = (f32[8,16,256]{2,1,0:T(8,128)S(1)}, f32[8,16,256]{2,1,0:T(8,128)}, u32[]{:S(2)}) copy-start(f32[8,16,256]{2,1,0:T(8,128)} %get-tuple-element.5) | copy-start | bytes 393220
where the time goes:
time: 86 us; the launch traced here: 85.8 us
  Pallas kernels  82.7 us (96%)
  local copies, waits for them, and re-layouts  2.46 us (3%)
    pallas_call x1, Pallas kernels, on_device(): pl.pallas_call(functools.partial(kernel, dims), out_shape=(jax.ShapeDtype...  82.7 us
    unnamed x4, local copies, waits for them, and re-layouts  2.46 us

commit v1 on v0

--- a/solution.py
+++ b/solution.py
@@ -23,6 +23,17 @@
      WP, WM, AP, AD, DC, LY, LW, RB,
      isend, irecv, psend, precv, msend, mrecv, rsend, rrecv) = refs
     gx, gy = lax.axis_index("gx"), lax.axis_index("gy")
+    local = [pltpu.make_async_copy(src, dst, lsem.at[n]) for n, (src, dst) in enumerate((
+        (ids_hbm, ids), (p_hbm, PX.at[0, pl.ds(1, nx)]), (d_hbm, MX.at[0, :, pl.ds(1, nx)]),
+        (p_hbm, p_old), (fs_hbm, fsource), (bf_hbm, bforce)))]
+    for copy in local:
+        copy.start()
+    barrier = pltpu.get_barrier_semaphore()
+    me, ndev = gx * ngy + gy, ngx * ngy
+
+    def peer(d):
+        t = lax.rem(me + d, ndev)
+        return lax.div(t, ngy), lax.rem(t, ngy)
     has = {(-1, 0): gx > 0, (1, 0): gx < ngx - 1, (0, -1): gy > 0, (0, 1): gy < ngy - 1}
     has[(1, -1)] = jnp.logical_and(has[(1, 0)], has[(0, -1)])
     has[(-1, 1)] = jnp.logical_and(has[(-1, 0)], has[(0, 1)])
@@ -98,14 +109,14 @@
         return copies_of(
             [(PX.at[f, 1], PX.at[f, nx + 1], (-1, 0)), (PX.at[f, nx], PX.at[f, 0], (1, 0)),
              (PYS.at[f, 0], PYH.at[f, 1], (0, -1)), (PYS.at[f, 1], PYH.at[f, 0], (0, 1))],
-            psend.at[f], precv.at[f])
+            psend.at[f % 2], precv.at[f % 2])
 
     def vector_field(f):
         return copies_of(
             [(MX.at[f, :, 1], MX.at[f, :, nx + 1], (-1, 0)), (MX.at[f, :, nx], MX.at[f, :, 0], (1, 0)),
              (MYS.at[f, 0], MYH.at[f, 1], (0, -1)), (MYS.at[f, 1], MYH.at[f, 0], (0, 1)),
              (MCS.at[f, 0], MCH.at[f, 0], (1, -1)), (MCS.at[f, 1], MCH.at[f, 1], (-1, 1))],
-            msend.at[f], mrecv.at[f])
+            msend.at[f % 2], mrecv.at[f % 2])
 
     def put_scalar(f, i, v):
         PX[f, i + 1] = v
@@ -121,12 +132,6 @@
     def put_corners(f):
         MCS[f, 0] = MX[f, 1, nx, 0:1, :]
         MCS[f, 1] = MX[f, 0, 1, ny - 1:ny, :]
-
-    local = [pltpu.make_async_copy(src, dst, lsem.at[n]) for n, (src, dst) in enumerate((
-        (ids_hbm, ids), (p_hbm, PX.at[0, pl.ds(1, nx)]), (d_hbm, MX.at[0, :, pl.ds(1, nx)]),
-        (p_hbm, p_old), (fs_hbm, fsource), (bf_hbm, bforce)))]
-    for copy in local:
-        copy.start()
 
     nf = 1 + OUTER * INNER
     XI[0] = jnp.zeros((ny, nz), jnp.int32)
@@ -145,15 +150,9 @@
                 MYH[f, s, a] = zero8
         return c
     lax.fori_loop(0, nf, clear, 0)
-
-    barrier = pltpu.get_barrier_semaphore()
-    me, ndev = gx * ngy + gy, ngx * ngy
-
-    def peer(d):
-        t = lax.rem(me + d, ndev)
-        return lax.div(t, ngy), lax.rem(t, ngy)
     for d in range(1, ndev):
         pl.semaphore_signal(barrier, inc=1, device_id=peer(d), device_id_type=MESH)
+
 
     def stage(i, c):
         code = ids[i] + 1
@@ -316,16 +315,17 @@
         for k, s in enumerate(sums):
             row = jnp.where(lane1 == k, jnp.sum(s, keepdims=True), row)
         RB[q, me] = row
-        made = []
         for d in sorted(range(1, ndev), key=lambda d: -min(d, ndev - d)):
             copy = pltpu.make_async_remote_copy(
-                src_ref=RB.at[q, me], dst_ref=RB.at[q, me], send_sem=rsend.at[q, d],
-                recv_sem=rrecv.at[q, d], device_id=peer(d), device_id_type=MESH)
+                src_ref=RB.at[q, me], dst_ref=RB.at[q, me], send_sem=rsend.at[q],
+                recv_sem=rrecv.at[q], device_id=peer(d), device_id_type=MESH)
             copy.start()
-            made.append(copy)
-        for copy in made:
-            copy.wait_recv()
-        summed.extend(made)
+        every = RB.at[q, pl.ds(0, ndev - 1)]
+        whole = pltpu.make_async_remote_copy(
+            src_ref=every, dst_ref=every, send_sem=rsend.at[q], recv_sem=rrecv.at[q],
+            device_id=peer(1), device_id_type=MESH)
+        whole.wait_recv()
+        summed.append(whole)
         parts = [RB[q, d] for d in range(ndev)]
         while len(parts) > 1:
             parts = [sum(parts[d + 1:d + 2], parts[d]) for d in range(0, len(parts), 2)]
@@ -365,7 +365,11 @@
     local[3].wait()
     local[4].wait()
 
-    sent = []
+    psent, msent = [], []
+
+    def retire(queue):
+        if len(queue) == 2:
+            wait_send(queue.pop(0))
     for outer in range(OUTER):
         base = 1 + INNER * outer
 
@@ -378,10 +382,11 @@
             u = r * PINV[i]
             put_scalar(base, i, u)
             return acc + fold(r * u)
+        retire(psent)
         made = scalar_field(base)
         n0 = loop(p_start, zacc, half=functools.partial(start, made, True))
         start(made, False)
-        sent.append(made)
+        psent.append(made)
         if outer > 0:
             loop(m_after, 0)
         if outer == 0:
@@ -409,12 +414,13 @@
                 return even, c[1] + fold(u * w)
             half = None
             if k < INNER - 1:
+                retire(psent)
                 made = scalar_field(base + k + 1)
                 half = functools.partial(start, made, True)
             sums += apply_pressure(base + k, p_step, (zacc,) * (1 if k == INNER - 1 else 2), half)
             if k < INNER - 1:
                 start(made, False)
-                sent.append(made)
+                psent.append(made)
         cs = combine(all_sum(2 * outer, sums))
 
         def p_update(j, c):
@@ -438,6 +444,7 @@
             u = block_solve(i, r)
             put_vector(base, i, u)
             return acc + dot3(r, u)
+        retire(msent)
         made = vector_field(base)
 
         def send_planes(f, made):
@@ -445,7 +452,7 @@
             start(made, True)
         n0 = loop(m_start, zacc, half=functools.partial(send_planes, base, made))
         start(made, False)
-        sent.append(made)
+        msent.append(made)
 
         def p_after(i, c):
             if outer == OUTER - 1:
@@ -475,12 +482,13 @@
                 return even, c[1] + dot3(u, w)
             half = None
             if k < INNER - 1:
+                retire(msent)
                 made = vector_field(base + k + 1)
                 half = functools.partial(send_planes, base + k + 1, made)
             sums += apply_mech(base + k, m_step, (zacc,) * (1 if k == INNER - 1 else 2), half)
             if k < INNER - 1:
                 start(made, False)
-                sent.append(made)
+                msent.append(made)
         cs = combine(all_sum(2 * outer + 1, sums))
 
         def mixed(get, cs=cs, base=base):
@@ -512,7 +520,7 @@
         if outer == OUTER - 1:
             loop(m_after, 0)
 
-    for made in sent:
+    for made in psent + msent:
         wait_send(made)
     for copy in summed:
         copy.wait_send()
@@ -541,8 +549,8 @@
         vm(nf, 3, *ext), vm(nf, 2, 3, *strip), vm(nf, 2, 3, *strip), vm(nf, 2, 1, nz), vm(nf, 2, 1, nz),
         vm(INNER, *cell), vm(INNER, 3, *cell), vm(*cell), vm(3, *cell), vm(*cell),
         vm(*strip), vm(*cell), vm(nq, ngx * ngy, 1, 128),
-        dma((4,)), dma((4,)), dma((nf, 4)), dma((nf, 4)), dma((nf, 6)), dma((nf, 6)),
-        dma((nq, ngx * ngy)), dma((nq, ngx * ngy)),
+        dma((4,)), dma((4,)), dma((2, 4)), dma((2, 4)), dma((2, 6)), dma((2, 6)),
+        dma((nq,)), dma((nq,)),
     ]
     block = pl.BlockSpec(memory_space=pltpu.VMEM)
     return pl.pallas_call(

time: 86 us -> 82.6 us (0.960)
  Pallas kernels: 82.7 us -> 79.3 us
    pallas_call x1, Pallas kernels: 82.7 us -> 79.3 us  [on_device(): pl.pallas_call(functools.partial(kernel, dims), out_shape=(jax.ShapeDtype...]
where the time goes in v1:
time: 82.6 us; the launch traced here: 82.4 us
  Pallas kernels  79.3 us (96%)
  local copies, waits for them, and re-layouts  2.46 us (3%)
    pallas_call x1, Pallas kernels, on_device(): pl.pallas_call(functools.partial(kernel, dims), out_shape=(jax.ShapeDtype...  79.3 us
    unnamed x4, local copies, waits for them, and re-layouts  2.46 us

profile of v1, /device:TPU:0, one launch (start us, length us, event | category | flops | bytes accessed | tf_op | source)
XLA Modules:
  0.0 82.4 jit_solution(16457384931860252613)
XLA Ops:
  0.6 79.3 %poro.1 = (f32[3,8,16,256]{3,2,1,0:T(8,128)}, f32[8,16,256]{2,1,0:T(8,128)}) custom-call(f32[5,8]{1,0:T(8,128)} %refs_0_.1, f32[3,8,16,256]{3,2,1,0:T(8,128)} %refs_1_.1, f32[8,16,256]{2,1,0:T(8,128)} %refs_2_.1, f32[3,8,16,256]{3,2,1,0:T(8,128)} %refs_3_.1, f32[8,16,256]{2,1,0:T(8,128)} %refs_4_.1, s32[8,16,256]{2,1,0:T(8,128)} %refs_5_.1), custom_call_target="tpu_custom_call" | custom-call | tf_op jit(solution)/shard_map/poro/pallas_call | solution.py:556
  79.9 0.0 copy-start
  79.9 1.8 %copy.10 = f32[3,8,16,256]{3,2,1,0:T(8,128)} copy(f32[3,8,16,256]{3,2,1,0:T(8,128)} %get-tuple-element.4) | data formatting | bytes 786432
  81.7 0.0 copy-done
  81.7 0.7 copy.11
Async XLA Ops:
  79.9 1.8 %copy-start = (f32[8,16,256]{2,1,0:T(8,128)S(1)}, f32[8,16,256]{2,1,0:T(8,128)}, u32[]{:S(2)}) copy-start(f32[8,16,256]{2,1,0:T(8,128)} %get-tuple-element.5) | copy-start | bytes 393220

commit v2 on v1

--- a/solution.py
+++ b/solution.py
@@ -9,6 +9,10 @@
 OUTER = 2
 INNER = 3
 step_time = 4.0
+D = INNER
+TINY = 1e-30
+VMEM_BYTES = 67043328
+DIAGONALS = ((1, -1), (-1, 1), (1, 1), (-1, -1))
 MESH = pl.DeviceIdType.MESH
 F32 = jnp.float32
 
@@ -17,14 +21,14 @@
     ngx, ngy, nx, ny, nz, nmat = dims
     (mat, d_hbm, p_hbm, bf_hbm, fs_hbm, ids_hbm, d_out, p_out,
      p_old, bforce, fsource, ids, lsem,
-     XI, YIS, YIH, LAM, SHR, PRM, BIO, LAMY, SHRY, PRMY, BIOY, STO, STAB,
+     XI, XIY, XIS, XIR, LAM, SHR, PRM, BIO, STO, STAB, LAMY,
      SX, SY, SZ, SSUM, FX, FY, FZ, DIAG, PINV, HB, KF,
-     PX, PYS, PYH, MX, MYS, MYH, MCS, MCH,
+     P0, P0Y, U, UY, UCS, UCR, MX, MYS, MYH, MCS, MCH,
      WP, WM, AP, AD, DC, LY, LW, RB,
-     isend, irecv, psend, precv, msend, mrecv, rsend, rrecv) = refs
+     isend, irecv, zsend, zrecv, psend, precv, msend, mrecv, rsend, rrecv) = refs
     gx, gy = lax.axis_index("gx"), lax.axis_index("gy")
     local = [pltpu.make_async_copy(src, dst, lsem.at[n]) for n, (src, dst) in enumerate((
-        (ids_hbm, ids), (p_hbm, PX.at[0, pl.ds(1, nx)]), (d_hbm, MX.at[0, :, pl.ds(1, nx)]),
+        (ids_hbm, ids), (p_hbm, P0.at[pl.ds(D, nx), pl.ds(0, ny)]), (d_hbm, MX.at[0, :, pl.ds(1, nx)]),
         (p_hbm, p_old), (fs_hbm, fsource), (bf_hbm, bforce)))]
     for copy in local:
         copy.start()
@@ -35,8 +39,8 @@
         t = lax.rem(me + d, ndev)
         return lax.div(t, ngy), lax.rem(t, ngy)
     has = {(-1, 0): gx > 0, (1, 0): gx < ngx - 1, (0, -1): gy > 0, (0, 1): gy < ngy - 1}
-    has[(1, -1)] = jnp.logical_and(has[(1, 0)], has[(0, -1)])
-    has[(-1, 1)] = jnp.logical_and(has[(-1, 0)], has[(0, 1)])
+    for c in DIAGONALS:
+        has[c] = jnp.logical_and(has[(c[0], 0)], has[(0, c[1])])
 
     rows = lax.broadcasted_iota(jnp.int32, (ny, nz), 0)
     lanes = lax.broadcasted_iota(jnp.int32, (ny, nz), 1)
@@ -46,6 +50,10 @@
     first_row, last_row = rows == 0, rows == ny - 1
     first_lane, last_lane = lanes == 0, lanes == nz - 1
     zero = jnp.zeros((ny, nz), F32)
+    near = lax.broadcasted_iota(jnp.int32, (8, nz), 0) < 4
+    wide = ny + 8
+    first_wide = lax.broadcasted_iota(jnp.int32, (wide, nz), 1) == 0
+    last_wide = lax.broadcasted_iota(jnp.int32, (wide, nz), 1) == nz - 1
     zero8 = jnp.zeros((nx, nz), F32)
 
     def upz(v):
@@ -59,6 +67,12 @@
 
     def dny(v, halo):
         return jnp.where(first_row, halo, pltpu.roll(v, 1, 0))
+
+    def upw(v):
+        return pltpu.roll(v, wide - 1, 0)
+
+    def dnw(v):
+        return pltpu.roll(v, 1, 0)
 
     def fold(v):
         out = None
@@ -105,11 +119,48 @@
             def _(copy=copy):
                 copy.wait_send()
 
-    def scalar_field(f):
-        return copies_of(
-            [(PX.at[f, 1], PX.at[f, nx + 1], (-1, 0)), (PX.at[f, nx], PX.at[f, 0], (1, 0)),
-             (PYS.at[f, 0], PYH.at[f, 1], (0, -1)), (PYS.at[f, 1], PYH.at[f, 0], (0, 1))],
-            psend.at[f % 2], precv.at[f % 2])
+    def wide_field(F, Y, CS, CR, depth, send, recv):
+        pairs = [(F.at[pl.ds(D, depth), pl.ds(0, ny)], F.at[pl.ds(D + nx, depth), pl.ds(0, ny)], (-1, 0)),
+                 (F.at[pl.ds(D + nx - depth, depth), pl.ds(0, ny)], F.at[pl.ds(D - depth, depth), pl.ds(0, ny)], (1, 0)),
+                 (F.at[pl.ds(D, nx), pl.ds(0, 8)], Y.at[1], (0, -1)),
+                 (F.at[pl.ds(D, nx), pl.ds(ny - 8, 8)], Y.at[0], (0, 1))]
+        if CS is not None:
+            pairs += [(CS.at[c], CR.at[c], off) for c, off in enumerate(DIAGONALS)]
+        return copies_of(pairs, send, recv)
+
+    def stage_corners(F, CS):
+        n, m = CS.shape[1:3]
+        for c, (sx, sy) in enumerate(DIAGONALS):
+            for t in range(n):
+                CS[c, t] = F[D + (t if sx < 0 else nx - n + t), (0 if sy < 0 else ny - m):(m if sy < 0 else ny), :]
+
+    def clear_missing(F, Y, CR, depth):
+        none = jnp.zeros((wide, nz), F.dtype)
+        for side, low in ((-1, D - depth), (1, D + nx)):
+            @pl.when(jnp.logical_not(has[(side, 0)]))
+            def _(low=low):
+                for t in range(depth):
+                    F[low + t] = none
+        for side, s in ((-1, 0), (1, 1)):
+            @pl.when(jnp.logical_not(has[(0, side)]))
+            def _(s=s):
+                for i in range(nx):
+                    Y[s, i] = none[:8]
+        if CR is not None:
+            for c, off in enumerate(DIAGONALS):
+                @pl.when(jnp.logical_not(has[(-off[0], -off[1])]))
+                def _(c=c):
+                    CR[c] = jnp.zeros(CR.shape[1:], F.dtype)
+
+    def merge(F, Y, CR):
+        for i in range(nx):
+            F[D + i, ny:, :] = jnp.where(near, Y[1, i], Y[0, i])
+        if CR is not None:
+            n, m = CR.shape[1:3]
+            for c, (sx, sy) in enumerate(DIAGONALS):
+                for t in range(n):
+                    low = ny if sy < 0 else wide - m
+                    F[(D + nx + t) if sx < 0 else (D - n + t), low:low + m, :] = CR[c, t]
 
     def vector_field(f):
         return copies_of(
@@ -118,11 +169,6 @@
              (MCS.at[f, 0], MCH.at[f, 0], (1, -1)), (MCS.at[f, 1], MCH.at[f, 1], (-1, 1))],
             msend.at[f % 2], mrecv.at[f % 2])
 
-    def put_scalar(f, i, v):
-        PX[f, i + 1] = v
-        PYS[f, 0, slice(i, i + 1), :] = v[0:1]
-        PYS[f, 1, slice(i, i + 1), :] = v[ny - 1:ny]
-
     def put_vector(f, i, vs):
         for a in range(3):
             MX[f, a, i + 1] = vs[a]
@@ -134,16 +180,8 @@
         MCS[f, 1] = MX[f, 0, 1, ny - 1:ny, :]
 
     nf = 1 + OUTER * INNER
-    XI[0] = jnp.zeros((ny, nz), jnp.int32)
-    XI[nx + 1] = jnp.zeros((ny, nz), jnp.int32)
-    for s in range(2):
-        YIH[s] = jnp.zeros((nx, nz), jnp.int32)
-
     def clear(f, c):
-        PX[f, 0] = zero
-        PX[f, nx + 1] = zero
         for s in range(2):
-            PYH[f, s] = zero8
             MCH[f, s] = jnp.zeros((1, nz), F32)
             for a in range(3):
                 MX[f, a, s * (nx + 1)] = zero
@@ -154,34 +192,30 @@
         pl.semaphore_signal(barrier, inc=1, device_id=peer(d), device_id_type=MESH)
 
 
-    def stage(i, c):
-        code = ids[i] + 1
-        XI[i + 1] = code
-        YIS[0, slice(i, i + 1), :] = code[0:1]
-        YIS[1, slice(i, i + 1), :] = code[ny - 1:ny]
-        return c
-
     def stage_values(i, c):
         for side, y in ((0, 0), (1, ny - 1)):
-            PYS[0, side, i:i + 1, :] = PX[0, i + 1, y:y + 1, :]
             for a in range(3):
                 MYS[0, side, a, i:i + 1, :] = MX[0, a, i + 1, y:y + 1, :]
         return c
     local[0].wait()
-    loop(stage, 0)
+    for i in range(nx):
+        XI[D + i, 0:ny, :] = ids[i] + 1
+    stage_corners(XI, XIS)
     local[1].wait()
+    pl.semaphore_wait(barrier, ndev - 1)
+    p_copy = wide_field(P0, P0Y, None, None, 1, zsend, zrecv)
+    codes_copy = wide_field(XI, XIY, XIS, XIR, D, isend, irecv)
+    d_copy = vector_field(0)
+    start(p_copy)
+    start(codes_copy)
     local[2].wait()
     loop(stage_values, 0)
     put_corners(0)
-    pl.semaphore_wait(barrier, ndev - 1)
-
-    codes_copy = copies_of(
-        [(XI.at[1], XI.at[nx + 1], (-1, 0)), (XI.at[nx], XI.at[0], (1, 0)),
-         (YIS.at[0], YIH.at[1], (0, -1)), (YIS.at[1], YIH.at[0], (0, 1))], isend, irecv)
-    p_copy, d_copy = scalar_field(0), vector_field(0)
-    start(codes_copy)
-    start(p_copy)
     start(d_copy)
+    clear_missing(XI, XIY, XIR, D)
+    clear_missing(P0, P0Y, None, 1)
+    for outer in range(OUTER):
+        clear_missing(U.at[INNER * outer], UY.at[outer], UCR.at[outer], D)
 
     def lookup(code, table_rows):
         out = [jnp.zeros(code.shape, F32) for _ in table_rows]
@@ -190,56 +224,64 @@
             out = [jnp.where(hit, mat[t, m], v) for t, v in zip(table_rows, out)]
         return out
 
-    def look_plane(i, c):
-        lam, shr, prm, sto, bio = lookup(XI[i + 1], (0, 1, 2, 3, 4))
+    def look(j, part):
+        code = XI[j, part, :]
+        lam, shr, prm, sto, bio = lookup(code, (0, 1, 2, 3, 4))
         bio = 0.25 * bio
-        LAM[i + 1] = lam
-        SHR[i + 1] = shr
-        PRM[i + 1] = prm
-        BIO[i + 1] = bio
-        STO[i] = sto
-        STAB[i] = bio * bio / (lam + 2.0 / 3.0 * shr)
+        LAM[j, part, :] = lam
+        SHR[j, part, :] = shr
+        PRM[j, part, :] = prm
+        BIO[j, part, :] = bio
+        STO[j, part, :] = sto
+        STAB[j, part, :] = bio * bio / jnp.maximum(lam + 2.0 / 3.0 * shr, TINY)
+    for i in range(nx):
+        look(D + i, slice(0, ny))
+    wait_recv(codes_copy)
+    merge(XI, XIY, XIR)
+    for i in range(nx):
+        look(D + i, slice(ny, wide))
+    for j in (D - 1, D + nx):
+        look(j, slice(0, wide))
+
+    def harmonic(one, two):
+        return (2.0 * step_time) * one * two / jnp.maximum(one + two, TINY)
+
+    def flow(j):
+        prm = PRM[j]
+        fzu = jnp.where(last_wide, 0.0, harmonic(prm, upz(prm)))
+        fyu = harmonic(prm, upw(prm))
+        FY[j], FZ[j] = fyu, fzu
+        diag = STO[j] + STAB[j] + (FX[j] + FX[j + 1] + fyu + dnw(fyu) + fzu + dnz(fzu))
+        DIAG[j] = diag
+        PINV[j] = jnp.where(XI[j] > 0, 1.0 / jnp.maximum(diag, TINY), 0.0)
+
+    def face(j):
+        FX[j] = harmonic(PRM[j - 1], PRM[j])
+    for j in range(D, D + nx + 1):
+        face(j)
+    for j in range(D, D + nx):
+        flow(j)
+
+    def rim():
+        outer_planes = [j for j in range(nx + 2 * D) if j < D - 1 or j > D + nx]
+        for j in outer_planes:
+            look(j, slice(0, wide))
+        for j in list(range(1, D)) + list(range(D + nx + 1, nx + 2 * D)):
+            face(j)
+        for j in list(range(1, D)) + list(range(D + nx, nx + 2 * D - 1)):
+            flow(j)
+
+    def stiff_face(j, c):
+        SX[j] = 0.5 * (SHR[D + j - 1, 0:ny, :] + SHR[D + j, 0:ny, :])
         return c
-    loop(look_plane, 0)
-    wait_recv(codes_copy)
-
-    for j in (0, nx + 1):
-        lam, shr, prm, bio = lookup(XI[j], (0, 1, 2, 4))
-        LAM[j] = lam
-        SHR[j] = shr
-        PRM[j] = prm
-        BIO[j] = 0.25 * bio
-    for s in range(2):
-        lam, shr, prm, bio = lookup(YIH[s], (0, 1, 2, 4))
-        SHRY[s] = shr
-        PRMY[s] = prm
-        if s == 0:
-            LAMY[...] = lam
-            BIOY[...] = 0.25 * bio
-
-    def harmonic(one, two):
-        return (2.0 * step_time) * one * two / (one + two)
-
-    def harmonic_plane(j, c):
-        FX[j] = harmonic(PRM[j], PRM[j + 1])
-        SX[j] = 0.5 * (SHR[j] + SHR[j + 1])
-        return c
-    loop(harmonic_plane, 0, 0, nx + 1)
 
     def coefs(i, c):
-        shr, prm, lam = SHR[i + 1], PRM[i + 1], LAM[i + 1]
-        row = slice(i, i + 1)
-        fyu = harmonic(prm, upy(prm, PRMY[1, row, :]))
-        fyd = harmonic(prm, dny(prm, PRMY[0, row, :]))
-        fzu = jnp.where(last_lane, 0.0, harmonic(prm, upz(prm)))
-        fzd = jnp.where(first_lane, 0.0, dnz(fzu))
-        FY[1, i], FY[0, i], FZ[1, i], FZ[0, i] = fyu, fyd, fzu, fzd
-        diag = STO[i] + STAB[i] + (FX[i] + FX[i + 1] + fyu + fyd + fzu + fzd)
-        DIAG[i] = diag
-        PINV[i] = 1.0 / diag
+        shrw, lamw = SHR[D + i], LAM[D + i]
+        shr, lam = shrw[:ny], lamw[:ny]
+        LAMY[slice(i, i + 1), :] = LAM[D + i, wide - 1:wide, :]
         half = 0.5 * shr
-        syu = 0.5 * (shr + upy(shr, SHRY[1, row, :]))
-        syd = 0.5 * (shr + dny(shr, SHRY[0, row, :]))
+        syw = 0.5 * (shrw + upw(shrw))
+        syu, syd = syw[:ny], dnw(syw)[:ny]
         szu = half + jnp.where(last_lane, 0.0, 0.5 * upz(shr))
         szd = half + jnp.where(first_lane, 0.0, 0.5 * dnz(shr))
         total = SX[i] + SX[i + 1] + syu + syd + szu + szd
@@ -247,23 +289,19 @@
         SZ[1, i] = jnp.where(last_lane, 0.0, szu)
         SZ[0, i] = jnp.where(first_lane, 0.0, szd)
         SSUM[i] = total
-        h0 = 1.0 / (total + LAM[i])
-        h1 = 1.0 / (total + dny(lam, LAMY[row, :]))
+        h0 = 1.0 / (total + LAM[D + i - 1, 0:ny, :])
+        h1 = 1.0 / (total + dnw(lamw)[:ny])
         h2 = 1.0 / (total + jnp.where(first_lane, 0.0, dnz(lam)))
         HB[0, i], HB[1, i], HB[2, i] = h0, h1, h2
         KF[i] = lam / (1.0 + lam * (h0 + h1 + h2))
         return c
-    loop(coefs, 0)
-
-    def apply_pressure(f, emit, init, half=None):
-        def body(i, c):
-            row = slice(i, i + 1)
-            v = PX[f, i + 1]
-            out = (DIAG[i] * v - FX[i + 1] * PX[f, i + 2] - FX[i] * PX[f, i]
-                   - FY[1, i] * upy(v, PYH[f, 1, row, :]) - FY[0, i] * dny(v, PYH[f, 0, row, :])
-                   - FZ[1, i] * upz(v) - FZ[0, i] * dnz(v))
-            return emit(i, v, out, c)
-        return loop(body, init, half=half)
+
+    def apply_pressure(F, j, rows):
+        v = F[j]
+        out = (DIAG[j] * v - FX[j + 1] * F[j + 1] - FX[j] * F[j - 1]
+               - FY[j] * upw(v) - dnw(FY[j] * v)
+               - FZ[j] * upz(v) - dnz(FZ[j] * v))
+        return v[:rows], out[:rows]
 
     def apply_mech(f, emit, init, half=None):
         m = [MYH[f, 0, a] for a in range(3)]
@@ -271,12 +309,12 @@
         z8 = jnp.where(lanes8 == nz - 1, 0.0, pltpu.roll(m[2], nz - 1, 1))
         LY[...] = LAMY[...] * (ahead - m[0] + MYS[f, 0, 1] - m[1] + z8 - m[2])
         m = [MX[f, a, 0] for a in range(3)]
-        below_first = LAM[0] * (MX[f, 0, 1] - m[0] + upy(m[1], MCH[f, 0]) - m[1]
+        below_first = LAM[D - 1, 0:ny, :] * (MX[f, 0, 1] - m[0] + upy(m[1], MCH[f, 0]) - m[1]
                           + jnp.where(last_lane, 0.0, upz(m[2])) - m[2])
 
         def weigh(i):
             w = [MX[f, a, i + 1] for a in range(3)]
-            return LAM[i + 1] * (MX[f, 0, i + 2] - w[0] + upy(w[1], MYH[f, 1, 1, i:i + 1, :]) - w[1]
+            return LAM[D + i, 0:ny, :] * (MX[f, 0, i + 2] - w[0] + upy(w[1], MYH[f, 1, 1, i:i + 1, :]) - w[1]
                                  + jnp.where(last_lane, 0.0, upz(w[2])) - w[2])
 
         def body(i, c):
@@ -292,7 +330,7 @@
                 div = part if div is None else div + part
                 ws.append(w)
                 outs.append(out)
-            weighted = LAM[i + 1] * div
+            weighted = LAM[D + i, 0:ny, :] * div
             LW[i] = weighted
             before = below_first if i == 0 else weigh(i - 1) if i == nx - 1 else LW[i - 1]
             below = (before, dny(weighted, LY[row, :]), jnp.where(first_lane, 0.0, dnz(weighted)))
@@ -350,13 +388,10 @@
 
     zacc = jnp.zeros((8, 128), F32)
     wait_recv(p_copy)
+    merge(P0, P0Y, None)
+    for i in range(nx):
+        AP[i] = apply_pressure(P0, D + i, ny)[1]
     wait_send(p_copy)
-    wait_send(codes_copy)
-
-    def keep_ap(i, v, out, c):
-        AP[i] = out
-        return c
-    apply_pressure(0, keep_ap, 0)
 
     def clear_change(i, c):
         DC[i] = zero
@@ -365,7 +400,7 @@
     local[3].wait()
     local[4].wait()
 
-    psent, msent = [], []
+    msent = []
 
     def retire(queue):
         if len(queue) == 2:
@@ -373,23 +408,30 @@
     for outer in range(OUTER):
         base = 1 + INNER * outer
 
+        u0 = U.at[INNER * outer]
+
         def p_start(i, acc):
             if outer > 0:
                 m_change(i, 0)
-            rhs = (STO[i] * p_old[i] + step_time * fsource[i] - BIO[i + 1] * DC[i]
-                   + STAB[i] * PX[0, i + 1])
+            own = slice(0, ny)
+            rhs = (STO[D + i, own, :] * p_old[i] + step_time * fsource[i] - BIO[D + i, own, :] * DC[i]
+                   + STAB[D + i, own, :] * P0[D + i, own, :])
             r = rhs - AP[i]
-            u = r * PINV[i]
-            put_scalar(base, i, u)
+            u = r * PINV[D + i, own, :]
+            u0[D + i, own, :] = u
             return acc + fold(r * u)
-        retire(psent)
-        made = scalar_field(base)
-        n0 = loop(p_start, zacc, half=functools.partial(start, made, True))
-        start(made, False)
-        psent.append(made)
+        if outer > 0:
+            wait_send(made_p)
+        n0 = loop(p_start, zacc)
+        stage_corners(u0, UCS.at[outer])
+        made_p = wide_field(u0, UY.at[outer], UCS.at[outer], UCR.at[outer], D, psend, precv)
+        start(made_p)
         if outer > 0:
             loop(m_after, 0)
         if outer == 0:
+            rim()
+            loop(stiff_face, 0, 0, nx + 1)
+            loop(coefs, 0)
             wait_recv(d_copy)
             wait_send(d_copy)
 
@@ -400,46 +442,38 @@
             apply_mech(0, keep_ad, 0)
             local[5].wait()
         sums = [n0]
+        wait_recv(made_p)
+        merge(u0, UY.at[outer], UCR.at[outer])
         for k in range(INNER):
             sums = [jnp.sum(v, keepdims=True) for v in sums]
-            wait_recv(made)
-
-            def p_step(i, v, w, c):
-                WP[k, i] = w
-                even = c[0] + fold(v * w)
-                if k == INNER - 1:
-                    return (even,)
-                u = w * PINV[i] - v
-                put_scalar(base + k + 1, i, u)
-                return even, c[1] + fold(u * w)
-            half = None
-            if k < INNER - 1:
-                retire(psent)
-                made = scalar_field(base + k + 1)
-                half = functools.partial(start, made, True)
-            sums += apply_pressure(base + k, p_step, (zacc,) * (1 if k == INNER - 1 else 2), half)
-            if k < INNER - 1:
-                start(made, False)
-                psent.append(made)
+            F = U.at[INNER * outer + k]
+            reach = 0 if k == INNER - 1 else D - 1 - k
+            even, odd = zacc, zacc
+            for j in range(D - reach, D + nx + reach):
+                own = D <= j < D + nx
+                v, w = apply_pressure(F, j, wide if k < INNER - 1 else ny)
+                if own:
+                    WP[k, j - D] = w[:ny]
+                    even = even + fold(v[:ny] * w[:ny])
+                if k < INNER - 1:
+                    u = w * PINV[j] - v
+                    U[INNER * outer + k + 1, j] = u
+                    if own:
+                        odd = odd + fold(u[:ny] * w[:ny])
+            sums += [even] if k == INNER - 1 else [even, odd]
         cs = combine(all_sum(2 * outer, sums))
 
-        def p_update(j, c):
-            v = PX[0, j]
+        for j in range(D - 1, D + nx):
+            v = P0[j]
             for k in range(INNER):
-                v = v + cs[k] * PX[base + k, j]
-            PX[0, j] = v
-            return c
-        loop(p_update, 0, 0, nx + 1)
-        ph = PYH[0, 0]
-        for k in range(INNER):
-            ph = ph + cs[k] * PYH[base + k, 0]
-        PYH[0, 0] = ph
-        LY[...] = BIOY[...] * ph
+                v = v + cs[k] * U[INNER * outer + k, j]
+            P0[j] = v
 
         def m_start(i, acc):
-            row = slice(i, i + 1)
-            load = BIO[i + 1] * PX[0, i + 1]
-            below = (BIO[i] * PX[0, i], dny(load, LY[row, :]), jnp.where(first_lane, 0.0, dnz(load)))
+            loadw = BIO[D + i] * P0[D + i]
+            load = loadw[:ny]
+            below = (BIO[D + i - 1, 0:ny, :] * P0[D + i - 1, 0:ny, :], dnw(loadw)[:ny],
+                     jnp.where(first_lane, 0.0, dnz(load)))
             r = [bforce[a, i] + (below[a] - load) - AD[a, i] for a in range(3)]
             u = block_solve(i, r)
             put_vector(base, i, u)
@@ -456,7 +490,7 @@
 
         def p_after(i, c):
             if outer == OUTER - 1:
-                p_out[i] = PX[0, i + 1]
+                p_out[i] = P0[D + i, 0:ny, :]
             else:
                 v = AP[i]
                 for k in range(INNER):
@@ -520,7 +554,7 @@
         if outer == OUTER - 1:
             loop(m_after, 0)
 
-    for made in psent + msent:
+    for made in msent + [codes_copy, made_p]:
         wait_send(made)
     for copy in summed:
         copy.wait_send()
@@ -536,31 +570,35 @@
     plane, strip = (ny, nz), (nx, nz)
     cell = (nx, ny, nz)
     ext = (nx + 2, ny, nz)
+    big = (nx + 2 * D, ny + 8, nz)
+    edge = (2, nx, 8, nz)
+    corner = (4, D - 1, 2 if D == 3 else 4, nz)
     dma = pltpu.SemaphoreType.DMA
     scratch = [
         vm(*cell), vm(3, *cell), vm(*cell), vm(*cell, dtype=jnp.int32), dma((6,)),
-        vm(*ext, dtype=jnp.int32), vm(2, *strip, dtype=jnp.int32), vm(2, *strip, dtype=jnp.int32),
-        vm(*ext), vm(*ext), vm(*ext), vm(*ext), vm(*strip), vm(2, *strip), vm(2, *strip), vm(*strip),
-        vm(*cell), vm(*cell),
+        vm(*big, dtype=jnp.int32), vm(*edge, dtype=jnp.int32),
+        vm(*corner, dtype=jnp.int32), vm(*corner, dtype=jnp.int32),
+        vm(*big), vm(*big), vm(*big), vm(*big), vm(*big), vm(*big), vm(*strip),
         vm(nx + 1, *plane), vm(2, *cell), vm(2, *cell), vm(*cell),
-        vm(nx + 1, *plane), vm(2, *cell), vm(2, *cell), vm(*cell), vm(*cell),
+        vm(*big), vm(*big), vm(*big), vm(*big), vm(*big),
         vm(3, *cell), vm(*cell),
-        vm(nf, *ext), vm(nf, 2, *strip), vm(nf, 2, *strip),
+        vm(*big), vm(*edge), vm(OUTER * INNER, *big), vm(OUTER, *edge), vm(OUTER, *corner), vm(OUTER, *corner),
         vm(nf, 3, *ext), vm(nf, 2, 3, *strip), vm(nf, 2, 3, *strip), vm(nf, 2, 1, nz), vm(nf, 2, 1, nz),
         vm(INNER, *cell), vm(INNER, 3, *cell), vm(*cell), vm(3, *cell), vm(*cell),
         vm(*strip), vm(*cell), vm(nq, ngx * ngy, 1, 128),
-        dma((4,)), dma((4,)), dma((2, 4)), dma((2, 4)), dma((2, 6)), dma((2, 6)),
+        dma((8,)), dma((8,)), dma((4,)), dma((4,)), dma((8,)), dma((8,)), dma((2, 6)), dma((2, 6)),
         dma((nq,)), dma((nq,)),
     ]
     block = pl.BlockSpec(memory_space=pltpu.VMEM)
     return pl.pallas_call(
         functools.partial(kernel, dims),
-        out_shape=(jax.ShapeDtypeStruct(d_old.shape, F32), jax.ShapeDtypeStruct(p_old.shape, F32)),
+        out_shape=(pltpu.VMEM(d_old.shape, F32), pltpu.VMEM(p_old.shape, F32)),
         in_specs=[pl.BlockSpec(memory_space=pltpu.SMEM)] + [pl.BlockSpec(memory_space=pl.ANY)] * 5,
         out_specs=(block, block),
         scratch_shapes=scratch,
         compiler_params=pltpu.CompilerParams(
-            collective_id=0, has_side_effects=True, vmem_limit_bytes=63 * 1024 * 1024),
+            collective_id=0, has_side_effects=True,
+            vmem_limit_bytes=VMEM_BYTES - 4 * (d_old.size + p_old.size) - 131072),
         name="poro",
     )(materials, d_old, p_old, bforce, fsource, ids)
 

time: 82.6 us -> 72.2 us (0.87)
  Pallas kernels: 79.3 us -> 70 us
  local copies, waits for them, and re-layouts: 2.46 us -> 1.4 us
    pallas_call x1, Pallas kernels: 79.3 us -> 70 us  [on_device(): pl.pallas_call(functools.partial(kernel, dims), out_shape=(pltpu.VMEM(d_o...]
    unnamed x4 -> x2, local copies, waits for them, and re-layouts: 2.46 us -> 1.4 us
where the time goes in v2:
time: 72.2 us; the launch traced here: 72.1 us
  Pallas kernels  70 us (97%)
  local copies, waits for them, and re-layouts  1.4 us (2%)
    pallas_call x1, Pallas kernels, on_device(): pl.pallas_call(functools.partial(kernel, dims), out_shape=(pltpu.VMEM(d_o...  70 us

profile of v2, /device:TPU:0, one launch (start us, length us, event | category | flops | bytes accessed | tf_op | source)
XLA Modules:
  0.0 72.1 jit_solution(5382760422383270613)
XLA Ops:
  0.6 70.0 %poro.1 = (f32[3,8,16,256]{3,2,1,0:T(8,128)S(1)}, f32[8,16,256]{2,1,0:T(8,128)S(1)}) custom-call(f32[5,8]{1,0:T(8,128)} %refs_0_.1, f32[3,8,16,256]{3,2,1,0:T(8,128)} %refs_1_.1, f32[8,16,256]{2,1,0:T(8,128)} %refs_2_.1, f32[3,8,16,256]{3,2,1,0:T(8,128)} %refs_3_.1, f32[8,16,256]{2,1,0:T(8,128)} %refs_4_.1, s32[8,16,256]{2,1,0:T(8,128)} %refs_5_.1), custom_call_target="tpu_custom_call" | custom-call | tf_op jit(solution)/shard_map/poro/pallas_call | solution.py:593
  70.7 0.7 %copy.10 = f32[3,8,16,256]{3,2,1,0:T(8,128)} copy(f32[3,8,16,256]{3,2,1,0:T(8,128)S(1)} %get-tuple-element.2) | data formatting | bytes 786432
  71.4 0.7 copy.11

commit v3 on v2

--- a/solution.py
+++ b/solution.py
@@ -23,9 +23,9 @@
      p_old, bforce, fsource, ids, lsem,
      XI, XIY, XIS, XIR, LAM, SHR, PRM, BIO, STO, STAB, LAMY,
      SX, SY, SZ, SSUM, FX, FY, FZ, DIAG, PINV, HB, KF,
-     P0, P0Y, U, UY, UCS, UCR, MX, MYS, MYH, MCS, MCH,
+     P0, P0Y, P0S, P0R, U, UY, UCS, UCR, VY, VCS, VCR, RX, RY, RCS, RCR, MX, MYS, MYH, MCS, MCH,
      WP, WM, AP, AD, DC, LY, LW, RB,
-     isend, irecv, zsend, zrecv, psend, precv, msend, mrecv, rsend, rrecv) = refs
+     isend, irecv, zsend, zrecv, vsend, vrecv, wsend, wrecv, psend, precv, msend, mrecv, rsend, rrecv) = refs
     gx, gy = lax.axis_index("gx"), lax.axis_index("gy")
     local = [pltpu.make_async_copy(src, dst, lsem.at[n]) for n, (src, dst) in enumerate((
         (ids_hbm, ids), (p_hbm, P0.at[pl.ds(D, nx), pl.ds(0, ny)]), (d_hbm, MX.at[0, :, pl.ds(1, nx)]),
@@ -152,6 +152,84 @@
                 def _(c=c):
                     CR[c] = jnp.zeros(CR.shape[1:], F.dtype)
 
+    def late_field(o):
+        last = U.at[INNER * o + INNER - 1]
+        pairs = [(last.at[pl.ds(D + nx - 2, 1), pl.ds(0, ny)], last.at[pl.ds(D - 2, 1), pl.ds(0, ny)], (1, 0)),
+                 (last.at[pl.ds(D, nx), pl.ds(ny - 8, 8)], VY.at[o], (0, 1))]
+        pairs += [(VCS.at[o, c], VCR.at[o, c], off) for c, off in enumerate(DIAGONALS[:3])]
+        return copies_of(pairs, vsend, vrecv)
+
+    def stage_late(o):
+        for c, (sx, sy) in enumerate(DIAGONALS[:3]):
+            for k in range(1, INNER):
+                for t in range(2):
+                    VCS[o, c, k - 1, t] = U[INNER * o + k, D + (t if sx < 0 else nx - 2 + t),
+                                            (0 if sy < 0 else ny - 2):(2 if sy < 0 else ny), :]
+
+    def merge_late(o):
+        f = INNER * o + INNER - 1
+        for i in range(nx):
+            U[f, D + i, ny:, :] = jnp.where(near, U[f, D + i, ny:, :], VY[o, i])
+        for c, (sx, sy) in enumerate(DIAGONALS[:3]):
+            for k in range(1, INNER):
+                for t in range(2):
+                    low = ny if sy < 0 else wide - 2
+                    U[INNER * o + k, (D + nx + t) if sx < 0 else (D - 2 + t), low:low + 2, :] = VCR[o, c, k - 1, t]
+
+    def load_field(o):
+        F = RX.at[o]
+        pairs = [(F.at[:, pl.ds(1, 1), pl.ds(0, ny)], F.at[:, pl.ds(nx + 1, 1), pl.ds(0, ny)], (-1, 0)),
+                 (F.at[:, pl.ds(nx, 1), pl.ds(0, ny)], F.at[:, pl.ds(0, 1), pl.ds(0, ny)], (1, 0)),
+                 (F.at[:, pl.ds(1, nx), pl.ds(0, 8)], RY.at[o, 1], (0, -1)),
+                 (F.at[:, pl.ds(1, nx), pl.ds(ny - 8, 8)], RY.at[o, 0], (0, 1)),
+                 (RCS.at[o, 0], RCR.at[o, 0], DIAGONALS[0]), (RCS.at[o, 1], RCR.at[o, 1], DIAGONALS[1])]
+        return copies_of(pairs, wsend, wrecv)
+
+    def stage_load(o):
+        for a in range(3):
+            RCS[o, 0, a] = RX[o, a, nx, 0:1, :]
+            RCS[o, 1, a] = RX[o, a, 1, ny - 1:ny, :]
+
+    def merge_load(o):
+        for a in range(3):
+            for i in range(nx):
+                RX[o, a, i + 1, ny:, :] = jnp.where(near, RY[o, 1, a, i], RY[o, 0, a, i])
+            RX[o, a, 0, ny:ny + 1, :] = RCR[o, 0, a]
+            RX[o, a, nx + 1, wide - 1:wide, :] = RCR[o, 1, a]
+
+    def clear_late(o):
+        none = jnp.zeros((wide, nz), F32)
+
+        @pl.when(jnp.logical_not(has[(-1, 0)]))
+        def _():
+            U[INNER * o + INNER - 1, D - 2] = none
+            for a in range(3):
+                RX[o, a, 0] = none
+
+        @pl.when(jnp.logical_not(has[(1, 0)]))
+        def _():
+            for a in range(3):
+                RX[o, a, nx + 1] = none
+
+        @pl.when(jnp.logical_not(has[(0, -1)]))
+        def _():
+            for i in range(nx):
+                VY[o, i] = none[:8]
+                for a in range(3):
+                    RY[o, 0, a, i] = none[:8]
+
+        @pl.when(jnp.logical_not(has[(0, 1)]))
+        def _():
+            for i in range(nx):
+                for a in range(3):
+                    RY[o, 1, a, i] = none[:8]
+        for c, off in enumerate(DIAGONALS[:3]):
+            @pl.when(jnp.logical_not(has[(-off[0], -off[1])]))
+            def _(c=c):
+                VCR[o, c] = jnp.zeros(VCR.shape[2:], F32)
+                if c < 2:
+                    RCR[o, c] = jnp.zeros(RCR.shape[2:], F32)
+
     def merge(F, Y, CR):
         for i in range(nx):
             F[D + i, ny:, :] = jnp.where(near, Y[1, i], Y[0, i])
@@ -202,8 +280,9 @@
         XI[D + i, 0:ny, :] = ids[i] + 1
     stage_corners(XI, XIS)
     local[1].wait()
+    stage_corners(P0, P0S)
     pl.semaphore_wait(barrier, ndev - 1)
-    p_copy = wide_field(P0, P0Y, None, None, 1, zsend, zrecv)
+    p_copy = wide_field(P0, P0Y, P0S, P0R, 2, zsend, zrecv)
     codes_copy = wide_field(XI, XIY, XIS, XIR, D, isend, irecv)
     d_copy = vector_field(0)
     start(p_copy)
@@ -213,9 +292,10 @@
     put_corners(0)
     start(d_copy)
     clear_missing(XI, XIY, XIR, D)
-    clear_missing(P0, P0Y, None, 1)
+    clear_missing(P0, P0Y, P0R, 2)
     for outer in range(OUTER):
         clear_missing(U.at[INNER * outer], UY.at[outer], UCR.at[outer], D)
+        clear_late(outer)
 
     def lookup(code, table_rows):
         out = [jnp.zeros(code.shape, F32) for _ in table_rows]
@@ -271,30 +351,30 @@
         for j in list(range(1, D)) + list(range(D + nx, nx + 2 * D - 1)):
             flow(j)
 
-    def stiff_face(j, c):
-        SX[j] = 0.5 * (SHR[D + j - 1, 0:ny, :] + SHR[D + j, 0:ny, :])
-        return c
-
-    def coefs(i, c):
-        shrw, lamw = SHR[D + i], LAM[D + i]
-        shr, lam = shrw[:ny], lamw[:ny]
-        LAMY[slice(i, i + 1), :] = LAM[D + i, wide - 1:wide, :]
+    def stiff_face(t):
+        SX[t] = 0.5 * (SHR[D + t - 2] + SHR[D + t - 1])
+
+    def coefs(i):
+        shr, lam = SHR[D + i], LAM[D + i]
         half = 0.5 * shr
-        syw = 0.5 * (shrw + upw(shrw))
-        syu, syd = syw[:ny], dnw(syw)[:ny]
-        szu = half + jnp.where(last_lane, 0.0, 0.5 * upz(shr))
-        szd = half + jnp.where(first_lane, 0.0, 0.5 * dnz(shr))
-        total = SX[i] + SX[i + 1] + syu + syd + szu + szd
-        SY[1, i], SY[0, i] = syu, syd
-        SZ[1, i] = jnp.where(last_lane, 0.0, szu)
-        SZ[0, i] = jnp.where(first_lane, 0.0, szd)
-        SSUM[i] = total
-        h0 = 1.0 / (total + LAM[D + i - 1, 0:ny, :])
-        h1 = 1.0 / (total + dnw(lamw)[:ny])
-        h2 = 1.0 / (total + jnp.where(first_lane, 0.0, dnz(lam)))
-        HB[0, i], HB[1, i], HB[2, i] = h0, h1, h2
-        KF[i] = lam / (1.0 + lam * (h0 + h1 + h2))
-        return c
+        syu = 0.5 * (shr + upw(shr))
+        syd = dnw(syu)
+        szu = half + jnp.where(last_wide, 0.0, 0.5 * upz(shr))
+        szd = half + jnp.where(first_wide, 0.0, 0.5 * dnz(shr))
+        total = SX[i + 1] + SX[i + 2] + syu + syd + szu + szd
+        if 0 <= i < nx:
+            LAMY[slice(i, i + 1), :] = LAM[D + i, wide - 1:wide, :]
+            SY[1, i], SY[0, i] = syu[:ny], syd[:ny]
+            SZ[1, i] = jnp.where(last_lane, 0.0, szu[:ny])
+            SZ[0, i] = jnp.where(first_lane, 0.0, szd[:ny])
+            SSUM[i] = total[:ny]
+        inside = XI[D + i] > 0
+        hs = []
+        for a, below in enumerate((LAM[D + i - 1], dnw(lam), jnp.where(first_wide, 0.0, dnz(lam)))):
+            h = jnp.where(inside, 1.0 / jnp.maximum(total + below, TINY), 0.0)
+            HB[a, i + 1] = h
+            hs.append(h)
+        KF[i + 1] = lam / (1.0 + lam * (hs[0] + hs[1] + hs[2]))
 
     def apply_pressure(F, j, rows):
         v = F[j]
@@ -323,7 +403,7 @@
             for a in range(3):
                 w, wx = MX[f, a, i + 1], MX[f, a, i + 2]
                 wy, wz = upy(w, MYH[f, 1, a, row, :]), upz(w)
-                out = (SSUM[i] * w - SX[i + 1] * wx - SX[i] * MX[f, a, i]
+                out = (SSUM[i] * w - SX[i + 2, 0:ny, :] * wx - SX[i + 1, 0:ny, :] * MX[f, a, i]
                        - SY[1, i] * wy - SY[0, i] * dny(w, MYH[f, 0, a, row, :])
                        - SZ[1, i] * wz - SZ[0, i] * dnz(w))
                 part = (wx, wy, jnp.where(last_lane, 0.0, wz))[a] - w
@@ -338,17 +418,18 @@
             return emit(i, ws, outs, c)
         return loop(body, init, half=half)
 
-    def block_solve(i, r):
-        scaled = [r[a] * HB[a, i] for a in range(3)]
-        tail = KF[i] * (scaled[0] + scaled[1] + scaled[2])
-        return [scaled[a] - HB[a, i] * tail for a in range(3)]
+    def block_solve(i, r, rows):
+        part = slice(0, rows)
+        scaled = [r[a] * HB[a, i + 1, part, :] for a in range(3)]
+        tail = KF[i + 1, part, :] * (scaled[0] + scaled[1] + scaled[2])
+        return [scaled[a] - HB[a, i + 1, part, :] * tail for a in range(3)]
 
     def dot3(a, b):
         return fold(a[0] * b[0] + a[1] * b[1] + a[2] * b[2])
 
     summed = []
 
-    def all_sum(q, sums):
+    def all_sum(q, sums, meanwhile=None):
         row = jnp.zeros((1, 128), F32)
         for k, s in enumerate(sums):
             row = jnp.where(lane1 == k, jnp.sum(s, keepdims=True), row)
@@ -362,6 +443,8 @@
         whole = pltpu.make_async_remote_copy(
             src_ref=every, dst_ref=every, send_sem=rsend.at[q], recv_sem=rrecv.at[q],
             device_id=peer(1), device_id_type=MESH)
+        if meanwhile is not None:
+            meanwhile()
         whole.wait_recv()
         summed.append(whole)
         parts = [RB[q, d] for d in range(ndev)]
@@ -388,7 +471,7 @@
 
     zacc = jnp.zeros((8, 128), F32)
     wait_recv(p_copy)
-    merge(P0, P0Y, None)
+    merge(P0, P0Y, P0R)
     for i in range(nx):
         AP[i] = apply_pressure(P0, D + i, ny)[1]
     wait_send(p_copy)
@@ -430,17 +513,25 @@
             loop(m_after, 0)
         if outer == 0:
             rim()
-            loop(stiff_face, 0, 0, nx + 1)
-            loop(coefs, 0)
+            for t in range(nx + 3):
+                stiff_face(t)
+            for i in range(-1, nx + 1):
+                coefs(i)
             wait_recv(d_copy)
             wait_send(d_copy)
 
             def keep_ad(i, ws, outs, c):
                 for a in range(3):
                     AD[a, i] = outs[a]
+                    RX[0, a, i + 1, 0:ny, :] = bforce[a, i] - outs[a]
                 return c
+            local[5].wait()
             apply_mech(0, keep_ad, 0)
-            local[5].wait()
+        else:
+            wait_send(made_r)
+        stage_load(outer)
+        made_r = load_field(outer)
+        start(made_r)
         sums = [n0]
         wait_recv(made_p)
         merge(u0, UY.at[outer], UCR.at[outer])
@@ -461,32 +552,49 @@
                     if own:
                         odd = odd + fold(u[:ny] * w[:ny])
             sums += [even] if k == INNER - 1 else [even, odd]
-        cs = combine(all_sum(2 * outer, sums))
-
-        for j in range(D - 1, D + nx):
+            if k == INNER - 2:
+                if outer > 0:
+                    wait_send(made_v)
+                stage_late(outer)
+                made_v = late_field(outer)
+                start(made_v)
+
+        def arrivals():
+            wait_recv(made_r)
+            merge_load(outer)
+            wait_recv(made_v)
+            merge_late(outer)
+        cs = combine(all_sum(2 * outer, sums, arrivals))
+
+        for j in range(D - 2, D + nx + 1):
             v = P0[j]
             for k in range(INNER):
                 v = v + cs[k] * U[INNER * outer + k, j]
             P0[j] = v
 
-        def m_start(i, acc):
-            loadw = BIO[D + i] * P0[D + i]
-            load = loadw[:ny]
-            below = (BIO[D + i - 1, 0:ny, :] * P0[D + i - 1, 0:ny, :], dnw(loadw)[:ny],
-                     jnp.where(first_lane, 0.0, dnz(load)))
-            r = [bforce[a, i] + (below[a] - load) - AD[a, i] for a in range(3)]
-            u = block_solve(i, r)
-            put_vector(base, i, u)
-            return acc + dot3(r, u)
-        retire(msent)
-        made = vector_field(base)
+        n0 = zacc
+        for i in range(-1, nx + 1):
+            load = BIO[D + i] * P0[D + i]
+            below = (BIO[D + i - 1] * P0[D + i - 1], dnw(load), jnp.where(first_wide, 0.0, dnz(load)))
+            r = [RX[outer, a, i + 1] + (below[a] - load) for a in range(3)]
+            u = block_solve(i, r, wide)
+            if 0 <= i < nx:
+                put_vector(base, i, [v[:ny] for v in u])
+                for a in range(3):
+                    MYH[base, 1, a, i:i + 1, :] = u[a][ny:ny + 1]
+                    MYH[base, 0, a, i:i + 1, :] = u[a][wide - 1:wide]
+                n0 = n0 + dot3([v[:ny] for v in r], [v[:ny] for v in u])
+            else:
+                for a in range(3):
+                    MX[base, a, i + 1] = u[a][:ny]
+                if i < 0:
+                    MCH[base, 0] = u[1][ny:ny + 1]
+                else:
+                    MCH[base, 1] = u[0][wide - 1:wide]
 
         def send_planes(f, made):
             put_corners(f)
             start(made, True)
-        n0 = loop(m_start, zacc, half=functools.partial(send_planes, base, made))
-        start(made, False)
-        msent.append(made)
 
         def p_after(i, c):
             if outer == OUTER - 1:
@@ -501,7 +609,8 @@
         sums = [n0]
         for k in range(INNER):
             sums = [jnp.sum(v, keepdims=True) for v in sums]
-            wait_recv(made)
+            if k > 0:
+                wait_recv(made)
 
             def m_step(i, v, w, c):
                 if outer < OUTER - 1:
@@ -510,7 +619,7 @@
                 even = c[0] + dot3(v, w)
                 if k == INNER - 1:
                     return (even,)
-                z = block_solve(i, w)
+                z = block_solve(i, w, ny)
                 u = [z[a] - v[a] for a in range(3)]
                 put_vector(base + k + 1, i, u)
                 return even, c[1] + dot3(u, w)
@@ -549,12 +658,12 @@
                     v = AD[a, i]
                     for k in range(INNER):
                         v = v + cs[k] * WM[k, a, i]
-                    AD[a, i] = v
+                    RX[outer + 1, a, i + 1, 0:ny, :] = bforce[a, i] - v
             return c
         if outer == OUTER - 1:
             loop(m_after, 0)
 
-    for made in msent + [codes_copy, made_p]:
+    for made in msent + [codes_copy, made_p, made_r, made_v]:
         wait_send(made)
     for copy in summed:
         copy.wait_send()
@@ -570,6 +679,7 @@
     plane, strip = (ny, nz), (nx, nz)
     cell = (nx, ny, nz)
     ext = (nx + 2, ny, nz)
+    broad = (ny + 8, nz)
     big = (nx + 2 * D, ny + 8, nz)
     edge = (2, nx, 8, nz)
     corner = (4, D - 1, 2 if D == 3 else 4, nz)
@@ -579,14 +689,16 @@
         vm(*big, dtype=jnp.int32), vm(*edge, dtype=jnp.int32),
         vm(*corner, dtype=jnp.int32), vm(*corner, dtype=jnp.int32),
         vm(*big), vm(*big), vm(*big), vm(*big), vm(*big), vm(*big), vm(*strip),
-        vm(nx + 1, *plane), vm(2, *cell), vm(2, *cell), vm(*cell),
+        vm(nx + 3, *broad), vm(2, *cell), vm(2, *cell), vm(*cell),
         vm(*big), vm(*big), vm(*big), vm(*big), vm(*big),
-        vm(3, *cell), vm(*cell),
-        vm(*big), vm(*edge), vm(OUTER * INNER, *big), vm(OUTER, *edge), vm(OUTER, *corner), vm(OUTER, *corner),
+        vm(3, nx + 2, *broad), vm(nx + 2, *broad),
+        vm(*big), vm(*edge), vm(*corner), vm(*corner), vm(OUTER * INNER, *big), vm(OUTER, *edge), vm(OUTER, *corner), vm(OUTER, *corner),
+        vm(OUTER, nx, 8, nz), vm(OUTER, 3, INNER - 1, 2, 2, nz), vm(OUTER, 3, INNER - 1, 2, 2, nz),
+        vm(OUTER, 3, nx + 2, *broad), vm(OUTER, 2, 3, nx, 8, nz), vm(OUTER, 2, 3, 1, nz), vm(OUTER, 2, 3, 1, nz),
         vm(nf, 3, *ext), vm(nf, 2, 3, *strip), vm(nf, 2, 3, *strip), vm(nf, 2, 1, nz), vm(nf, 2, 1, nz),
         vm(INNER, *cell), vm(INNER, 3, *cell), vm(*cell), vm(3, *cell), vm(*cell),
         vm(*strip), vm(*cell), vm(nq, ngx * ngy, 1, 128),
-        dma((8,)), dma((8,)), dma((4,)), dma((4,)), dma((8,)), dma((8,)), dma((2, 6)), dma((2, 6)),
+        dma((8,)), dma((8,)), dma((8,)), dma((8,)), dma((5,)), dma((5,)), dma((6,)), dma((6,)), dma((8,)), dma((8,)), dma((2, 6)), dma((2, 6)),
         dma((nq,)), dma((nq,)),
     ]
     block = pl.BlockSpec(memory_space=pltpu.VMEM)

time: 72.2 us -> 68.8 us (0.953)
  Pallas kernels: 70 us -> 66.6 us
    pallas_call x1, Pallas kernels: 70 us -> 66.6 us  [on_device(): pl.pallas_call(functools.partial(kernel, dims), out_shape=(pltpu.VMEM(d_o...]
where the time goes in v3:
time: 68.8 us; the launch traced here: 68.7 us
  Pallas kernels  66.6 us (97%)
  local copies, waits for them, and re-layouts  1.4 us (2%)
    pallas_call x1, Pallas kernels, on_device(): pl.pallas_call(functools.partial(kernel, dims), out_shape=(pltpu.VMEM(d_o...  66.6 us
    unnamed x2, local copies, waits for them, and re-layouts  1.4 us

profile of v3, /device:TPU:0, one launch (start us, length us, event | category | flops | bytes accessed | tf_op | source)
XLA Modules:
  0.0 68.7 jit_solution(842463648939216252)
XLA Ops:
  0.6 66.6 %poro.1 = (f32[3,8,16,256]{3,2,1,0:T(8,128)S(1)}, f32[8,16,256]{2,1,0:T(8,128)S(1)}) custom-call(f32[5,8]{1,0:T(8,128)} %refs_0_.1, f32[3,8,16,256]{3,2,1,0:T(8,128)} %refs_1_.1, f32[8,16,256]{2,1,0:T(8,128)} %refs_2_.1, f32[3,8,16,256]{3,2,1,0:T(8,128)} %refs_3_.1, f32[8,16,256]{2,1,0:T(8,128)} %refs_4_.1, s32[8,16,256]{2,1,0:T(8,128)} %refs_5_.1), custom_call_target="tpu_custom_call" | custom-call | tf_op jit(solution)/shard_map/poro/pallas_call | solution.py:705
  67.3 0.7 %copy.10 = f32[3,8,16,256]{3,2,1,0:T(8,128)} copy(f32[3,8,16,256]{3,2,1,0:T(8,128)S(1)} %get-tuple-element.2) | data formatting | bytes 786432
  68.0 0.7 copy.11

commit v4 on v3

--- a/solution.py
+++ b/solution.py
@@ -24,7 +24,7 @@
      XI, XIY, XIS, XIR, LAM, SHR, PRM, BIO, STO, STAB, LAMY,
      SX, SY, SZ, SSUM, FX, FY, FZ, DIAG, PINV, HB, KF,
      P0, P0Y, P0S, P0R, U, UY, UCS, UCR, VY, VCS, VCR, RX, RY, RCS, RCR, MX, MYS, MYH, MCS, MCH,
-     WP, WM, AP, AD, DC, LY, LW, RB,
+     WP, WM, AP, AD, DC, DK, LY, LW, RB,
      isend, irecv, zsend, zrecv, vsend, vrecv, wsend, wrecv, psend, precv, msend, mrecv, rsend, rrecv) = refs
     gx, gy = lax.axis_index("gx"), lax.axis_index("gy")
     local = [pltpu.make_async_copy(src, dst, lsem.at[n]) for n, (src, dst) in enumerate((
@@ -127,6 +127,18 @@
         if CS is not None:
             pairs += [(CS.at[c], CR.at[c], off) for c, off in enumerate(DIAGONALS)]
         return copies_of(pairs, send, recv)
+
+    def split_field(F, Y, CS, CR, depth, send, recv):
+        far = depth - 1
+        pairs = [(F.at[pl.ds(D, 1), pl.ds(0, ny)], F.at[pl.ds(D + nx, 1), pl.ds(0, ny)], (-1, 0)),
+                 (F.at[pl.ds(D + nx - 1, 1), pl.ds(0, ny)], F.at[pl.ds(D - 1, 1), pl.ds(0, ny)], (1, 0)),
+                 (F.at[pl.ds(D, nx), pl.ds(0, 8)], Y.at[1], (0, -1)),
+                 (F.at[pl.ds(D, nx), pl.ds(ny - 8, 8)], Y.at[0], (0, 1)),
+                 (F.at[pl.ds(D + 1, far), pl.ds(0, ny)], F.at[pl.ds(D + nx + 1, far), pl.ds(0, ny)], (-1, 0)),
+                 (F.at[pl.ds(D + nx - depth, far), pl.ds(0, ny)], F.at[pl.ds(D - depth, far), pl.ds(0, ny)], (1, 0))]
+        pairs += [(CS.at[c], CR.at[c], off) for c, off in enumerate(DIAGONALS)]
+        made = copies_of(pairs, send, recv)
+        return made[:4], made[4:]
 
     def stage_corners(F, CS):
         n, m = CS.shape[1:3]
@@ -234,11 +246,14 @@
         for i in range(nx):
             F[D + i, ny:, :] = jnp.where(near, Y[1, i], Y[0, i])
         if CR is not None:
-            n, m = CR.shape[1:3]
-            for c, (sx, sy) in enumerate(DIAGONALS):
-                for t in range(n):
-                    low = ny if sy < 0 else wide - m
-                    F[(D + nx + t) if sx < 0 else (D - n + t), low:low + m, :] = CR[c, t]
+            merge_corners(F, CR)
+
+    def merge_corners(F, CR):
+        n, m = CR.shape[1:3]
+        for c, (sx, sy) in enumerate(DIAGONALS):
+            for t in range(n):
+                low = ny if sy < 0 else wide - m
+                F[(D + nx + t) if sx < 0 else (D - n + t), low:low + m, :] = CR[c, t]
 
     def vector_field(f):
         return copies_of(
@@ -258,14 +273,6 @@
         MCS[f, 1] = MX[f, 0, 1, ny - 1:ny, :]
 
     nf = 1 + OUTER * INNER
-    def clear(f, c):
-        for s in range(2):
-            MCH[f, s] = jnp.zeros((1, nz), F32)
-            for a in range(3):
-                MX[f, a, s * (nx + 1)] = zero
-                MYH[f, s, a] = zero8
-        return c
-    lax.fori_loop(0, nf, clear, 0)
     for d in range(1, ndev):
         pl.semaphore_signal(barrier, inc=1, device_id=peer(d), device_id_type=MESH)
 
@@ -282,20 +289,40 @@
     local[1].wait()
     stage_corners(P0, P0S)
     pl.semaphore_wait(barrier, ndev - 1)
-    p_copy = wide_field(P0, P0Y, P0S, P0R, 2, zsend, zrecv)
-    codes_copy = wide_field(XI, XIY, XIS, XIR, D, isend, irecv)
+    p_near, p_far = split_field(P0, P0Y, P0S, P0R, 2, zsend, zrecv)
+    codes_near, codes_far = split_field(XI, XIY, XIS, XIR, D, isend, irecv)
     d_copy = vector_field(0)
-    start(p_copy)
-    start(codes_copy)
+    start(p_near)
+    start(codes_near)
+    start(codes_far)
     local[2].wait()
     loop(stage_values, 0)
     put_corners(0)
     start(d_copy)
+    start(p_far)
     clear_missing(XI, XIY, XIR, D)
     clear_missing(P0, P0Y, P0R, 2)
     for outer in range(OUTER):
         clear_missing(U.at[INNER * outer], UY.at[outer], UCR.at[outer], D)
         clear_late(outer)
+
+    def clear_vector(f, c):
+        for side, j, s in ((-1, 0, 0), (1, nx + 1, 1)):
+            @pl.when(jnp.logical_not(has[(side, 0)]))
+            def _(j=j):
+                for a in range(3):
+                    MX[f, a, j] = zero
+
+            @pl.when(jnp.logical_not(has[(0, side)]))
+            def _(s=s):
+                for a in range(3):
+                    MYH[f, s, a] = zero8
+        for c2, off in enumerate(DIAGONALS[:2]):
+            @pl.when(jnp.logical_not(has[(-off[0], -off[1])]))
+            def _(c2=c2):
+                MCH[f, c2] = jnp.zeros((1, nz), F32)
+        return c
+    lax.fori_loop(0, nf, clear_vector, 0)
 
     def lookup(code, table_rows):
         out = [jnp.zeros(code.shape, F32) for _ in table_rows]
@@ -316,12 +343,12 @@
         STAB[j, part, :] = bio * bio / jnp.maximum(lam + 2.0 / 3.0 * shr, TINY)
     for i in range(nx):
         look(D + i, slice(0, ny))
-    wait_recv(codes_copy)
-    merge(XI, XIY, XIR)
+    wait_recv(codes_near)
+    merge(XI, XIY, None)
     for i in range(nx):
         look(D + i, slice(ny, wide))
     for j in (D - 1, D + nx):
-        look(j, slice(0, wide))
+        look(j, slice(0, ny))
 
     def harmonic(one, two):
         return (2.0 * step_time) * one * two / jnp.maximum(one + two, TINY)
@@ -343,12 +370,16 @@
         flow(j)
 
     def rim():
-        outer_planes = [j for j in range(nx + 2 * D) if j < D - 1 or j > D + nx]
-        for j in outer_planes:
-            look(j, slice(0, wide))
-        for j in list(range(1, D)) + list(range(D + nx + 1, nx + 2 * D)):
+        wait_recv(codes_far)
+        merge_corners(XI, XIR)
+        for j in (D - 1, D + nx):
+            look(j, slice(ny, wide))
+        for j in range(nx + 2 * D):
+            if j < D - 1 or j > D + nx:
+                look(j, slice(0, wide))
+        for j in list(range(1, D + 1)) + list(range(D + nx, nx + 2 * D)):
             face(j)
-        for j in list(range(1, D)) + list(range(D + nx, nx + 2 * D - 1)):
+        for j in list(range(1, D + 1)) + list(range(D + nx - 1, nx + 2 * D - 1)):
             flow(j)
 
     def stiff_face(t):
@@ -470,16 +501,11 @@
         return c0, c1, c2
 
     zacc = jnp.zeros((8, 128), F32)
-    wait_recv(p_copy)
-    merge(P0, P0Y, P0R)
+    wait_recv(p_near)
+    merge(P0, P0Y, None)
     for i in range(nx):
         AP[i] = apply_pressure(P0, D + i, ny)[1]
-    wait_send(p_copy)
-
-    def clear_change(i, c):
-        DC[i] = zero
-        return c
-    loop(clear_change, 0)
+
     local[3].wait()
     local[4].wait()
 
@@ -495,10 +521,12 @@
 
         def p_start(i, acc):
             if outer > 0:
-                m_change(i, 0)
+                m_change(i)
             own = slice(0, ny)
-            rhs = (STO[D + i, own, :] * p_old[i] + step_time * fsource[i] - BIO[D + i, own, :] * DC[i]
+            rhs = (STO[D + i, own, :] * p_old[i] + step_time * fsource[i]
                    + STAB[D + i, own, :] * P0[D + i, own, :])
+            if outer > 0:
+                rhs = rhs - BIO[D + i, own, :] * DC[i]
             r = rhs - AP[i]
             u = r * PINV[D + i, own, :]
             u0[D + i, own, :] = u
@@ -560,6 +588,11 @@
                 start(made_v)
 
         def arrivals():
+            if outer == 0:
+                wait_recv(p_far)
+                merge_corners(P0, P0R)
+                wait_send(p_near)
+                wait_send(p_far)
             wait_recv(made_r)
             merge_load(outer)
             wait_recv(made_v)
@@ -632,7 +665,13 @@
             if k < INNER - 1:
                 start(made, False)
                 msent.append(made)
-        cs = combine(all_sum(2 * outer + 1, sums))
+        def changes():
+            for k in range(INNER):
+                for i in range(nx):
+                    w = [MX[base + k, a, i + 1] for a in range(3)]
+                    DK[k, i] = (MX[base + k, 0, i + 2] - w[0] + upy(w[1], MYH[base + k, 1, 1, i:i + 1, :]) - w[1]
+                                + jnp.where(last_lane, 0.0, upz(w[2])) - w[2])
+        cs = combine(all_sum(2 * outer + 1, sums, changes if outer < OUTER - 1 else None))
 
         def mixed(get, cs=cs, base=base):
             v = cs[0] * get(base)
@@ -640,14 +679,12 @@
                 v = v + cs[k] * get(base + k)
             return v
 
-        def m_change(i, c):
-            row = slice(i, i + 1)
-            change = [mixed(lambda f, a=a: MX[f, a, i + 1]) for a in range(3)]
-            cx = mixed(lambda f: MX[f, 0, i + 2])
-            cy = upy(change[1], mixed(lambda f: MYH[f, 1, 1, row, :]))
-            cz = jnp.where(last_lane, 0.0, upz(change[2]))
-            DC[i] = DC[i] + (cx - change[0] + cy - change[1] + cz - change[2])
-            return c
+        def m_change(i, outer=outer, cs=cs):
+            v = DC[i] if outer > 0 else None
+            for k in range(INNER):
+                part = cs[k] * DK[k, i]
+                v = part if v is None else v + part
+            DC[i] = v
 
         def m_after(i, c, cs=cs, mixed=mixed, outer=outer):
             for a in range(3):
@@ -663,7 +700,7 @@
         if outer == OUTER - 1:
             loop(m_after, 0)
 
-    for made in msent + [codes_copy, made_p, made_r, made_v]:
+    for made in msent + [codes_near, codes_far, made_p, made_r, made_v]:
         wait_send(made)
     for copy in summed:
         copy.wait_send()
@@ -696,9 +733,9 @@
         vm(OUTER, nx, 8, nz), vm(OUTER, 3, INNER - 1, 2, 2, nz), vm(OUTER, 3, INNER - 1, 2, 2, nz),
         vm(OUTER, 3, nx + 2, *broad), vm(OUTER, 2, 3, nx, 8, nz), vm(OUTER, 2, 3, 1, nz), vm(OUTER, 2, 3, 1, nz),
         vm(nf, 3, *ext), vm(nf, 2, 3, *strip), vm(nf, 2, 3, *strip), vm(nf, 2, 1, nz), vm(nf, 2, 1, nz),
-        vm(INNER, *cell), vm(INNER, 3, *cell), vm(*cell), vm(3, *cell), vm(*cell),
+        vm(INNER, *cell), vm(INNER, 3, *cell), vm(*cell), vm(3, *cell), vm(*cell), vm(INNER, *cell),
         vm(*strip), vm(*cell), vm(nq, ngx * ngy, 1, 128),
-        dma((8,)), dma((8,)), dma((8,)), dma((8,)), dma((5,)), dma((5,)), dma((6,)), dma((6,)), dma((8,)), dma((8,)), dma((2, 6)), dma((2, 6)),
+        dma((10,)), dma((10,)), dma((10,)), dma((10,)), dma((5,)), dma((5,)), dma((6,)), dma((6,)), dma((8,)), dma((8,)), dma((2, 6)), dma((2, 6)),
         dma((nq,)), dma((nq,)),
     ]
     block = pl.BlockSpec(memory_space=pltpu.VMEM)

time: 68.8 us -> 67.6 us (0.983)
  Pallas kernels: 66.6 us -> 65.4 us
    pallas_call x1, Pallas kernels: 66.6 us -> 65.4 us  [on_device(): pl.pallas_call(functools.partial(kernel, dims), out_shape=(pltpu.VMEM(d_o...]
where the time goes in v4:
time: 67.6 us; the launch traced here: 67.5 us
  Pallas kernels  65.4 us (97%)
  local copies, waits for them, and re-layouts  1.4 us (2%)
    pallas_call x1, Pallas kernels, on_device(): pl.pallas_call(functools.partial(kernel, dims), out_shape=(pltpu.VMEM(d_o...  65.4 us
    unnamed x2, local copies, waits for them, and re-layouts  1.4 us

profile of v4, /device:TPU:0, one launch (start us, length us, event | category | flops | bytes accessed | tf_op | source)
XLA Modules:
  0.0 67.5 jit_solution(13801086453275932301)
XLA Ops:
  0.6 65.4 %poro.1 = (f32[3,8,16,256]{3,2,1,0:T(8,128)S(1)}, f32[8,16,256]{2,1,0:T(8,128)S(1)}) custom-call(f32[5,8]{1,0:T(8,128)} %refs_0_.1, f32[3,8,16,256]{3,2,1,0:T(8,128)} %refs_1_.1, f32[8,16,256]{2,1,0:T(8,128)} %refs_2_.1, f32[3,8,16,256]{3,2,1,0:T(8,128)} %refs_3_.1, f32[8,16,256]{2,1,0:T(8,128)} %refs_4_.1, s32[8,16,256]{2,1,0:T(8,128)} %refs_5_.1), custom_call_target="tpu_custom_call" | custom-call | tf_op jit(solution)/shard_map/poro/pallas_call | solution.py:742
  66.1 0.7 %copy.10 = f32[3,8,16,256]{3,2,1,0:T(8,128)} copy(f32[3,8,16,256]{3,2,1,0:T(8,128)S(1)} %get-tuple-element.2) | data formatting | bytes 786432
  66.8 0.7 copy.11

commit v5 on v4

--- a/solution.py
+++ b/solution.py
@@ -19,8 +19,8 @@
 
 def kernel(dims, *refs):
     ngx, ngy, nx, ny, nz, nmat = dims
-    (mat, d_hbm, p_hbm, bf_hbm, fs_hbm, ids_hbm, d_out, p_out,
-     p_old, bforce, fsource, ids, lsem,
+    (mat_hbm, d_hbm, p_hbm, bf_hbm, fs_hbm, ids_hbm, d_out, p_out,
+     mat, p_old, bforce, fsource, ids, lsem,
      XI, XIY, XIS, XIR, LAM, SHR, PRM, BIO, STO, STAB, LAMY,
      SX, SY, SZ, SSUM, FX, FY, FZ, DIAG, PINV, HB, KF,
      P0, P0Y, P0S, P0R, U, UY, UCS, UCR, VY, VCS, VCR, RX, RY, RCS, RCR, MX, MYS, MYH, MCS, MCH,
@@ -29,7 +29,7 @@
     gx, gy = lax.axis_index("gx"), lax.axis_index("gy")
     local = [pltpu.make_async_copy(src, dst, lsem.at[n]) for n, (src, dst) in enumerate((
         (ids_hbm, ids), (p_hbm, P0.at[pl.ds(D, nx), pl.ds(0, ny)]), (d_hbm, MX.at[0, :, pl.ds(1, nx)]),
-        (p_hbm, p_old), (fs_hbm, fsource), (bf_hbm, bforce)))]
+        (p_hbm, p_old), (fs_hbm, fsource), (bf_hbm, bforce), (mat_hbm, mat)))]
     for copy in local:
         copy.start()
     barrier = pltpu.get_barrier_semaphore()
@@ -341,6 +341,7 @@
         BIO[j, part, :] = bio
         STO[j, part, :] = sto
         STAB[j, part, :] = bio * bio / jnp.maximum(lam + 2.0 / 3.0 * shr, TINY)
+    local[6].wait()
     for i in range(nx):
         look(D + i, slice(0, ny))
     wait_recv(codes_near)
@@ -414,14 +415,24 @@
                - FZ[j] * upz(v) - dnz(FZ[j] * v))
         return v[:rows], out[:rows]
 
-    def apply_mech(f, emit, init, half=None):
-        m = [MYH[f, 0, a] for a in range(3)]
-        ahead = jnp.where(rows8 == nx - 1, MCH[f, 1], pltpu.roll(m[0], nx - 1, 0))
-        z8 = jnp.where(lanes8 == nz - 1, 0.0, pltpu.roll(m[2], nz - 1, 1))
-        LY[...] = LAMY[...] * (ahead - m[0] + MYS[f, 0, 1] - m[1] + z8 - m[2])
-        m = [MX[f, a, 0] for a in range(3)]
-        below_first = LAM[D - 1, 0:ny, :] * (MX[f, 0, 1] - m[0] + upy(m[1], MCH[f, 0]) - m[1]
-                          + jnp.where(last_lane, 0.0, upz(m[2])) - m[2])
+    def apply_mech(f, emit, init, half=None, late=None):
+        def below_y(corner):
+            m = [MYH[f, 0, a] for a in range(3)]
+            ahead = pltpu.roll(m[0], nx - 1, 0)
+            if corner:
+                ahead = jnp.where(rows8 == nx - 1, MCH[f, 1], ahead)
+            z8 = jnp.where(lanes8 == nz - 1, 0.0, pltpu.roll(m[2], nz - 1, 1))
+            LY[...] = LAMY[...] * (ahead - m[0] + MYS[f, 0, 1] - m[1] + z8 - m[2])
+
+        def below_x():
+            m = [MX[f, a, 0] for a in range(3)]
+            return LAM[D - 1, 0:ny, :] * (MX[f, 0, 1] - m[0] + upy(m[1], MCH[f, 0]) - m[1]
+                              + jnp.where(last_lane, 0.0, upz(m[2])) - m[2])
+
+        below_y(late is None)
+        edge = []
+        if late is None:
+            edge.append(below_x())
 
         def weigh(i):
             w = [MX[f, a, i + 1] for a in range(3)]
@@ -443,10 +454,19 @@
                 outs.append(out)
             weighted = LAM[D + i, 0:ny, :] * div
             LW[i] = weighted
-            before = below_first if i == 0 else weigh(i - 1) if i == nx - 1 else LW[i - 1]
+            before = edge[0] if i == 0 else weigh(i - 1) if i == nx - 1 or (i == 1 and late is not None) else LW[i - 1]
             below = (before, dny(weighted, LY[row, :]), jnp.where(first_lane, 0.0, dnz(weighted)))
             outs = [outs[a] + (below[a] - weighted) for a in range(3)]
             return emit(i, ws, outs, c)
+        if late is not None:
+            for i in range(1, nx - 1):
+                init = body(i, init)
+            late()
+            below_y(True)
+            edge.append(below_x())
+            for i in (0, nx - 1):
+                init = body(i, init)
+            return init
         return loop(body, init, half=half)
 
     def block_solve(i, r, rows):
@@ -561,14 +581,21 @@
         made_r = load_field(outer)
         start(made_r)
         sums = [n0]
-        wait_recv(made_p)
-        merge(u0, UY.at[outer], UCR.at[outer])
+        wait_recv(made_p[2:4])
+        merge(u0, UY.at[outer], None)
         for k in range(INNER):
             sums = [jnp.sum(v, keepdims=True) for v in sums]
             F = U.at[INNER * outer + k]
             reach = 0 if k == INNER - 1 else D - 1 - k
             even, odd = zacc, zacc
-            for j in range(D - reach, D + nx + reach):
+            planes = list(range(D - reach, D + nx + reach))
+            if k == 0:
+                inner = planes[reach + 1:-reach - 1]
+                planes = inner + [j for j in planes if j not in inner]
+            for n, j in enumerate(planes):
+                if k == 0 and n == len(inner):
+                    wait_recv(made_p[:2] + made_p[4:])
+                    merge_corners(u0, UCR.at[outer])
                 own = D <= j < D + nx
                 v, w = apply_pressure(F, j, wide if k < INNER - 1 else ny)
                 if own:
@@ -642,7 +669,11 @@
         sums = [n0]
         for k in range(INNER):
             sums = [jnp.sum(v, keepdims=True) for v in sums]
-            if k > 0:
+            late = None
+            if k == INNER - 1:
+                wait_recv(made[2:4])
+                late = functools.partial(wait_recv, made[:2] + made[4:])
+            elif k > 0:
                 wait_recv(made)
 
             def m_step(i, v, w, c):
@@ -661,7 +692,7 @@
                 retire(msent)
                 made = vector_field(base + k + 1)
                 half = functools.partial(send_planes, base + k + 1, made)
-            sums += apply_mech(base + k, m_step, (zacc,) * (1 if k == INNER - 1 else 2), half)
+            sums += apply_mech(base + k, m_step, (zacc,) * (1 if k == INNER - 1 else 2), half, late)
             if k < INNER - 1:
                 start(made, False)
                 msent.append(made)
@@ -722,7 +753,7 @@
     corner = (4, D - 1, 2 if D == 3 else 4, nz)
     dma = pltpu.SemaphoreType.DMA
     scratch = [
-        vm(*cell), vm(3, *cell), vm(*cell), vm(*cell, dtype=jnp.int32), dma((6,)),
+        pltpu.SMEM((5, nmat), F32), vm(*cell), vm(3, *cell), vm(*cell), vm(*cell, dtype=jnp.int32), dma((7,)),
         vm(*big, dtype=jnp.int32), vm(*edge, dtype=jnp.int32),
         vm(*corner, dtype=jnp.int32), vm(*corner, dtype=jnp.int32),
         vm(*big), vm(*big), vm(*big), vm(*big), vm(*big), vm(*big), vm(*strip),
@@ -742,7 +773,7 @@
     return pl.pallas_call(
         functools.partial(kernel, dims),
         out_shape=(pltpu.VMEM(d_old.shape, F32), pltpu.VMEM(p_old.shape, F32)),
-        in_specs=[pl.BlockSpec(memory_space=pltpu.SMEM)] + [pl.BlockSpec(memory_space=pl.ANY)] * 5,
+        in_specs=[pl.BlockSpec(memory_space=pl.ANY)] * 6,
         out_specs=(block, block),
         scratch_shapes=scratch,
         compiler_params=pltpu.CompilerParams(

time: 67.6 us -> 66.1 us (0.978)
  Pallas kernels: 65.4 us -> 63.9 us
    pallas_call x1, Pallas kernels: 65.4 us -> 63.9 us  [on_device(): pl.pallas_call(functools.partial(kernel, dims), out_shape=(pltpu.VMEM(d_o...]
where the time goes in v5:
time: 66.1 us; the launch traced here: 65.9 us
  Pallas kernels  63.9 us (97%)
  local copies, waits for them, and re-layouts  1.4 us (2%)
    pallas_call x1, Pallas kernels, on_device(): pl.pallas_call(functools.partial(kernel, dims), out_shape=(pltpu.VMEM(d_o...  63.9 us
    unnamed x2, local copies, waits for them, and re-layouts  1.4 us

profile of v5, /device:TPU:0, one launch (start us, length us, event | category | flops | bytes accessed | tf_op | source)
XLA Modules:
  0.0 65.9 jit_solution(3896611161421930530)
XLA Ops:
  0.6 63.9 %poro.1 = (f32[3,8,16,256]{3,2,1,0:T(8,128)S(1)}, f32[8,16,256]{2,1,0:T(8,128)S(1)}) custom-call(f32[5,8]{1,0:T(8,128)} %refs_0_.1, f32[3,8,16,256]{3,2,1,0:T(8,128)} %refs_1_.1, f32[8,16,256]{2,1,0:T(8,128)} %refs_2_.1, f32[3,8,16,256]{3,2,1,0:T(8,128)} %refs_3_.1, f32[8,16,256]{2,1,0:T(8,128)} %refs_4_.1, s32[8,16,256]{2,1,0:T(8,128)} %refs_5_.1), custom_call_target="tpu_custom_call" | custom-call | tf_op jit(solution)/shard_map/poro/pallas_call | solution.py:773
  64.5 0.7 %copy.10 = f32[3,8,16,256]{3,2,1,0:T(8,128)} copy(f32[3,8,16,256]{3,2,1,0:T(8,128)S(1)} %get-tuple-element.2) | data formatting | bytes 786432
  65.3 0.7 copy.11

commit v6 on v5

--- a/solution.py
+++ b/solution.py
@@ -344,12 +344,10 @@
     local[6].wait()
     for i in range(nx):
         look(D + i, slice(0, ny))
-    wait_recv(codes_near)
+    wait_recv(codes_near[2:])
     merge(XI, XIY, None)
     for i in range(nx):
         look(D + i, slice(ny, wide))
-    for j in (D - 1, D + nx):
-        look(j, slice(0, ny))
 
     def harmonic(one, two):
         return (2.0 * step_time) * one * two / jnp.maximum(one + two, TINY)
@@ -365,9 +363,16 @@
 
     def face(j):
         FX[j] = harmonic(PRM[j - 1], PRM[j])
-    for j in range(D, D + nx + 1):
+    for j in range(D + 1, D + nx):
         face(j)
-    for j in range(D, D + nx):
+    for j in range(D + 1, D + nx - 1):
+        flow(j)
+    wait_recv(codes_near[:2])
+    for j in (D - 1, D + nx):
+        look(j, slice(0, ny))
+    for j in (D, D + nx):
+        face(j)
+    for j in (D, D + nx - 1):
         flow(j)
 
     def rim():

time: 66.1 us -> 66.1 us (level)
  no operation moved by 1% of the time
where the time goes in v6:
time: 66.1 us; the launch traced here: 65.9 us
  Pallas kernels  63.9 us (97%)
  local copies, waits for them, and re-layouts  1.4 us (2%)
    pallas_call x1, Pallas kernels, on_device(): pl.pallas_call(functools.partial(kernel, dims), out_shape=(pltpu.VMEM(d_o...  63.9 us
    unnamed x2, local copies, waits for them, and re-layouts  1.4 us

profile of v6, /device:TPU:0, one launch (start us, length us, event | category | flops | bytes accessed | tf_op | source)
XLA Modules:
  0.0 65.9 jit_solution(9372004257285305976)
XLA Ops:
  0.6 63.9 %poro.1 = (f32[3,8,16,256]{3,2,1,0:T(8,128)S(1)}, f32[8,16,256]{2,1,0:T(8,128)S(1)}) custom-call(f32[5,8]{1,0:T(8,128)} %refs_0_.1, f32[3,8,16,256]{3,2,1,0:T(8,128)} %refs_1_.1, f32[8,16,256]{2,1,0:T(8,128)} %refs_2_.1, f32[3,8,16,256]{3,2,1,0:T(8,128)} %refs_3_.1, f32[8,16,256]{2,1,0:T(8,128)} %refs_4_.1, s32[8,16,256]{2,1,0:T(8,128)} %refs_5_.1), custom_call_target="tpu_custom_call" | custom-call | tf_op jit(solution)/shard_map/poro/pallas_call | solution.py:778
  64.5 0.7 %copy.10 = f32[3,8,16,256]{3,2,1,0:T(8,128)} copy(f32[3,8,16,256]{3,2,1,0:T(8,128)S(1)} %get-tuple-element.2) | data formatting | bytes 786432
  65.3 0.7 copy.11
